TPU v7x, 8 devices: a whole 2x2x1 slice. The times are simulated.
8 devices in a mesh: depth: 2 (over z, y), col: 2 (over x), row: 2 (over core).
Axes of the slice: x: 2, y: 2, z: 1, core: 2. Of those that a mesh axis runs over, the one named last changes fastest.
Arguments:
- tokens: bfloat16 [4096, 4096], P(('depth', 'row'), 'col')
- w_up: bfloat16 [4096, 16384], P('row', 'col')
- w_down: bfloat16 [16384, 4096], P('row', 'col')
- grad_out: bfloat16 [4096, 4096], P(('depth', 'row'), 'col')
Outputs:
- output 1: bfloat16 [4096, 4096], P(('depth', 'row'), 'col')
- output 2: bfloat16 [4096, 4096], P(('depth', 'row'), 'col')
- output 3: float32 [4096, 16384], P('row', 'col')
- output 4: float32 [16384, 4096], P('row', 'col')
All inputs are finite; a program needn't handle non-finite values.
Results may differ from a plain program's by a relative error of at most 0.001.
Values are sent between devices in bfloat16 or wider.
A program may use at most 1 GiB of HBM per device.

v0:
```python
import math
import jax
import jax.numpy as jnp
from jax import lax
from jax.sharding import PartitionSpec as P, NamedSharding

INV_ROOT_TWO = 1.0 / math.sqrt(2.0)
INV_ROOT_TAU = 1.0 / math.sqrt(2.0 * math.pi)


def gelu_value(pre_act):
    return 0.5 * pre_act * (1.0 + lax.erf(pre_act * INV_ROOT_TWO))


def gelu_slope(pre_act):
    return 0.5 * (1.0 + lax.erf(pre_act * INV_ROOT_TWO)) + pre_act * jnp.exp(-0.5 * pre_act * pre_act) * INV_ROOT_TAU


def solution(mesh):
    act_spec = P(("depth", "row"), "col")
    wgt_spec = P("row", "col")

    def grid_block(tok_blk, up_blk, down_blk, grad_blk):
        tok_rows = lax.all_gather(tok_blk, "col", axis=1, tiled=True)
        up_cols = lax.all_gather(up_blk, "row", axis=0, tiled=True)
        down_cols = lax.all_gather(down_blk, "row", axis=0, tiled=True)
        pre_act = jnp.einsum("th,hf->tf", tok_rows, up_cols, preferred_element_type=jnp.float32)
        hidden_act = gelu_value(pre_act).astype(jnp.bfloat16)
        act_rows = lax.all_gather(hidden_act, "col", axis=1, tiled=True)
        out_blk = jnp.einsum("tf,fh->th", act_rows, down_cols, preferred_element_type=jnp.float32).astype(jnp.bfloat16)
        act_part = jnp.einsum("th,fh->tf", grad_blk, down_cols, preferred_element_type=jnp.float32)
        grad_act = lax.psum_scatter(act_part, "col", scatter_dimension=1, tiled=True)
        grad_pre = (grad_act * gelu_slope(pre_act)).astype(jnp.bfloat16)
        tok_part = jnp.einsum("tf,hf->th", grad_pre, up_cols, preferred_element_type=jnp.float32)
        grad_tok = lax.psum_scatter(tok_part, "col", scatter_dimension=1, tiled=True).astype(jnp.bfloat16)
        down_part = jnp.einsum("tf,th->fh", act_rows, grad_blk, preferred_element_type=jnp.float32)
        down_sum = lax.psum(lax.psum_scatter(down_part, "row", scatter_dimension=0, tiled=True), "depth")
        up_part = jnp.einsum("th,tf->hf", tok_rows, grad_pre, preferred_element_type=jnp.float32)
        up_sum = lax.psum(lax.psum_scatter(up_part, "row", scatter_dimension=0, tiled=True), "depth")
        return out_blk, grad_tok, up_sum, down_sum

    return jax.shard_map(grid_block, mesh=mesh, in_specs=(act_spec, wgt_spec, wgt_spec, act_spec), out_specs=(act_spec, act_spec, wgt_spec, wgt_spec), check_vma=False)
```

profile of v0, /device:TPU:0, one launch (start us, length us, event | category | flops | bytes accessed | tf_op | source)
XLA Modules:
  0.0 4949.6 jit_solution(1535226967106612788)
XLA Ops:
  7.2 0.0 all-gather.11.cloned.1.call-start
  7.2 0.7 all-gather.11.cloned.1.call-update
  7.9 0.0 all-gather.5.cloned.1.call-start
  7.9 0.7 all-gather.5.cloned.1.call-update
  8.6 0.0 all-gather.7.cloned.1.call-start
  8.7 0.7 all-gather.7.cloned.1.call-update
  9.4 0.0 reduce-scatter.8.cloned.1.call-start
  9.4 93.1 %all-gather.11.cloned.1.call-done = bf16[16384,2048]{1,0:T(8,128)(2,1)} async-done(((bf16[8192,2048]{1,0:T(8,128)(2,1)}), bf16[16384,2048]{1,0:T(8,128)(2,1)}) %all-gather.11.cloned.1.call-update) | async-done | bytes 67108880 | tf_op jit(solution)/shard_map/all_gather | solution.py:26
  102.6 78.8 %fusion.6 = f32[1024,16384]{1,0:T(8,128)} fusion(bf16[1024,2048]{1,0:T(8,128)(2,1)} %param.7, bf16[16384,2048]{1,0:T(8,128)(2,1)} %all-gather.11.cloned.1.call-done), kind=kOutput, calls=%fused_computation.11 | convolution fusion | flops 68719476736 | bytes 138412032 | tf_op jit(solution)/shard_map/th,fh->tf/dot_general | solution.py:31
  181.4 0.6 all-gather.9.cloned.1.call-start
  182.0 25.6 all-gather.5.cloned.1.call-done
  207.5 91.8 %all-gather.7.cloned.1.call-done = bf16[4096,8192]{1,0:T(8,128)(2,1)} async-done(((bf16[2048,8192]{1,0:T(8,128)(2,1)}), bf16[4096,8192]{1,0:T(8,128)(2,1)}) %all-gather.7.cloned.1.call-update) | async-done | bytes 67108880 | tf_op jit(solution)/shard_map/all_gather | solution.py:25
  299.3 729.5 %reduce-scatter.8.cloned.1.call-done = f32[1024,8192]{1,0:T(8,128)} async-done(((f32[1024,16384]{1,0:T(8,128)}), f32[1024,8192]{1,0:T(8,128)}) %reduce-scatter.8.cloned.1.call-update) | async-done | bytes 33554448 | tf_op jit(solution)/shard_map/reduce_scatter | solution.py:32
  1028.8 91.1 %fusion.5 = (bf16[1024,8192]{1,0:T(8,128)(2,1)}, bf16[1024,8192]{1,0:T(8,128)(2,1)}) fusion(f32[1024,8192]{1,0:T(8,128)} %reduce-scatter.8.cloned.1.call-done, bf16[1024,4096]{1,0:T(8,128)(2,1)} %all-gather.5.cloned.1.call-done, bf16[4096,8192]{1,0:T(8,128)(2,1)} %all-gather.7.cloned.1.call-done), kind=kOutput, calls=%fused_computation.7 | convolution fusion | flops 68828528640 | bytes 142606336 | tf_op jit(solution)/shard_map/th,hf->tf/dot_general | solution.py:27
  1119.9 0.2 reduce-scatter.12.cloned.1.call-start
  1120.2 81.5 %convolution_bitcast_fusion = f32[4096,8192]{0,1:T(8,128)} fusion(bf16[1024,8192]{1,0:T(8,128)(2,1)} %get-tuple-element.12, bf16[1024,4096]{1,0:T(8,128)(2,1)} %all-gather.5.cloned.1.call-done), kind=kOutput, calls=%fused_computation | convolution fusion | flops 68719476736 | bytes 159383552 | tf_op jit(solution)/shard_map/th,tf->hf/dot_general | solution.py:38
  1201.6 0.3 reduce-scatter.14.cloned.1.call-start
  1201.9 303.7 %all-gather.9.cloned.1.call-done = bf16[1024,16384]{1,0:T(8,128)(2,1)} async-done(((bf16[1024,8192]{1,0:T(8,128)(2,1)}), bf16[1024,16384]{1,0:T(8,128)(2,1)}) %all-gather.9.cloned.1.call-update) | async-done | bytes 33554448 | tf_op jit(solution)/shard_map/all_gather | solution.py:29
  1505.6 80.9 %fusion.8 = f32[16384,2048]{1,0:T(8,128)} fusion(bf16[1024,16384]{1,0:T(8,128)(2,1)} %all-gather.9.cloned.1.call-done, bf16[1024,2048]{1,0:T(8,128)(2,1)} %param.7), kind=kOutput, calls=%fused_computation.13 | convolution fusion | flops 68719476736 | bytes 171966464 | tf_op jit(solution)/shard_map/tf,th->fh/dot_general | solution.py:36
  1586.5 0.3 reduce-scatter.10.cloned.1.call-start
  1586.8 80.2 %fusion.7 = f32[1024,4096]{1,0:T(8,128)} fusion(bf16[1024,8192]{1,0:T(8,128)(2,1)} %get-tuple-element.12, bf16[4096,8192]{1,0:T(8,128)(2,1)} %all-gather.7.cloned.1.call-done), kind=kOutput, calls=%fused_computation.12 | convolution fusion | flops 68719476736 | bytes 100663296 | tf_op jit(solution)/shard_map/tf,hf->th/dot_general | solution.py:34
  1667.1 0.0 all-reduce.4.cloned.1.call-start
  1667.2 0.7 all-reduce.4.cloned.1.call-update
  1667.8 0.3 all-reduce.6.cloned.1.call-start
  1668.2 130.1 %reduce-scatter.14.cloned.1.call-done = f32[8192,2048]{1,0:T(8,128)} async-done(((f32[16384,2048]{1,0:T(8,128)}), f32[8192,2048]{1,0:T(8,128)}) %reduce-scatter.14.cloned.1.call-update) | async-done | bytes 67108880
  1798.3 190.3 %reduce-scatter.10.cloned.1.call-done = f32[1024,2048]{1,0:T(8,128)} async-done(((f32[1024,4096]{1,0:T(8,128)}), f32[1024,2048]{1,0:T(8,128)}) %reduce-scatter.10.cloned.1.call-update) | async-done | bytes 8388624 | tf_op jit(solution)/shard_map/reduce_scatter | solution.py:35
  1988.6 6.0 convert_element_type.15
  1994.6 78.5 %convolution_convert_fusion = bf16[1024,2048]{1,0:T(8,128)(2,1)} fusion(bf16[1024,16384]{1,0:T(8,128)(2,1)} %all-gather.9.cloned.1.call-done, bf16[16384,2048]{1,0:T(8,128)(2,1)} %all-gather.11.cloned.1.call-done), kind=kOutput, calls=%fused_computation.10 | convolution fusion | flops 68721573888 | bytes 104857600 | tf_op jit(solution)/shard_map/tf,fh->th/dot_general | solution.py:30
  2073.1 1369.4 %all-reduce.4.cloned.1.call-done = f32[2048,8192]{0,1:T(8,128)} async-done(((f32[2048,8192]{0,1:T(8,128)}), f32[2048,8192]{0,1:T(8,128)}) %all-reduce.4.cloned.1.call-update) | async-done | bytes 67108880 | tf_op jit(solution)/shard_map/psum | solution.py:39
  3442.5 61.2 %copy.9 = f32[2048,8192]{1,0:T(8,128)} copy(f32[2048,8192]{0,1:T(8,128)} %all-reduce.4.cloned.1.call-done) | data formatting | bytes 134217728
  3503.7 1394.8 %all-reduce.6.cloned.1.call-done = f32[8192,2048]{1,0:T(8,128)} async-done(((f32[8192,2048]{1,0:T(8,128)}), f32[8192,2048]{1,0:T(8,128)}) %all-reduce.6.cloned.1.call-update) | async-done | bytes 67108880 | tf_op jit(solution)/shard_map/psum | solution.py:37
  4898.5 43.8 copy.12
  (7 shorter events, 0.1 us)
Async XLA Ops:
  7.2 95.4 %all-gather.11.cloned.1.call-start = ((), (), s32[]{:S(2)}) async-start(), calls=%async_computation.7 | async-start | bytes 100663296 | tf_op jit(solution)/shard_map/all_gather | solution.py:26
  7.9 199.6 %all-gather.5.cloned.1.call-start = ((), (), s32[]{:S(2)}) async-start(), calls=%async_computation.4 | async-start | bytes 12582912 | tf_op jit(solution)/shard_map/all_gather | solution.py:24
  8.6 290.6 %all-gather.7.cloned.1.call-start = ((), (), s32[]{:S(2)}) async-start(), calls=%async_computation.5 | async-start | bytes 100663296 | tf_op jit(solution)/shard_map/all_gather | solution.py:25
  9.4 1019.4 %reduce-scatter.8.cloned.1.call-start = ((), (), s32[]{:S(2)}) async-start(), calls=%async_computation.8 | async-start | bytes 100663296 | tf_op jit(solution)/shard_map/reduce_scatter | solution.py:32
  181.4 1324.2 %all-gather.9.cloned.1.call-start = ((), (), s32[]{:S(2)}) async-start(), calls=%async_computation.6 | async-start | bytes 50331648 | tf_op jit(solution)/shard_map/all_gather | solution.py:29
  1119.9 547.2 %reduce-scatter.12.cloned.1.call-start = ((), (), s32[]{:S(2)}) async-start(), calls=%async_computation.10 | async-start | bytes 201326592 | tf_op jit(solution)/shard_map/reduce_scatter | solution.py:39
  1201.6 596.6 %reduce-scatter.14.cloned.1.call-start = ((), (), s32[]{:S(2)}) async-start(), calls=%async_computation.13 | async-start | bytes 201326592
  1586.5 402.0 %reduce-scatter.10.cloned.1.call-start = ((), (), s32[]{:S(2)}) async-start(), calls=%async_computation.9 | async-start | bytes 25165824 | tf_op jit(solution)/shard_map/reduce_scatter | solution.py:35
  1667.1 1775.4 %all-reduce.4.cloned.1.call-start = ((), (), s32[]{:S(2)}) async-start(), calls=%async_computation.11 | async-start | bytes 134217728 | tf_op jit(solution)/shard_map/psum | solution.py:39
  1667.8 3230.7 %all-reduce.6.cloned.1.call-start = ((), (), s32[]{:S(2)}) async-start(), calls=%async_computation.12 | async-start | bytes 134217728 | tf_op jit(solution)/shard_map/psum | solution.py:37
Sparse Core Ops, SparseCore 0:
  9.5 93.0 all-gather.10
  104.1 103.4 all-gather.4
  209.1 90.1 all-gather.6
  302.0 726.7 reduce-scatter.7
  1120.1 385.4 all-gather.8
  1507.7 143.5 reduce-scatter.11
  1653.5 144.6 reduce-scatter.13
  1801.1 187.4 reduce-scatter.9
  1991.0 1451.4 all-reduce.3
  3444.8 1453.6 all-reduce.5
where the time goes:
time: 4960 us; the launch traced here: 4950 us
  waiting for transfers between devices  4330 us (87%)
  matrix products  491 us (10%)
  local copies, waits for them, and re-layouts  105 us (2%)
    psum x1, waiting for transfers between devices, grid_block(): lax.psum(lax.psum_scatter(down_part, 'row', scatter_dimension=0, tiled=Tr...  1390 us
    psum x1, waiting for transfers between devices, grid_block(): lax.psum(lax.psum_scatter(up_part, 'row', scatter_dimension=0, tiled=True...  1370 us
    reduce_scatter x1, waiting for transfers between devices, grid_block(): lax.psum_scatter(act_part, 'col', scatter_dimension=1, tiled=True)  730 us
    all_gather x1, waiting for transfers between devices, grid_block(): act_rows = lax.all_gather(hidden_act, 'col', axis=1, tiled=True)  304 us
    reduce_scatter x1, waiting for transfers between devices, grid_block(): lax.psum_scatter(tok_part, 'col', scatter_dimension=1, tiled=True)  190 us
    unnamed x11, waiting for transfers between devices  133 us
    unnamed x2, local copies, waits for them, and re-layouts  105 us
  transfers between devices with their start and end apart: 10, of which 9 were waited for; matrix products, arithmetic and copies ran while one was open for 9% of the time, Pallas kernels for 0%

commit v1 on v0

v1 whole, which is shorter than its diff:
```python
import math
import jax
import jax.numpy as jnp
from jax import lax
from jax.sharding import PartitionSpec as P

INV_ROOT_TWO = 1.0 / math.sqrt(2.0)
INV_ROOT_TAU = 1.0 / math.sqrt(2.0 * math.pi)
SWAP = [(0, 1), (1, 0)]
PIECES = 4


def gelu_value(pre_act):
    return 0.5 * pre_act * (1.0 + lax.erf(pre_act * INV_ROOT_TWO))


def gelu_slope(pre_act):
    return 0.5 * (1.0 + lax.erf(pre_act * INV_ROOT_TWO)) + pre_act * jnp.exp(-0.5 * pre_act * pre_act) * INV_ROOT_TAU


def dot(a, b, eq, add=None):
    out = jnp.einsum(eq, a, b, preferred_element_type=jnp.float32)
    return lax.optimization_barrier(out if add is None else out + add)


def forward(a, b):
    pre = jnp.einsum("th,hf->tf", a, b, preferred_element_type=jnp.float32)
    return lax.optimization_barrier((pre, gelu_value(pre).astype(jnp.bfloat16)))


def backward(a, b, add, pre):
    out = jnp.einsum("th,fh->tf", a, b, preferred_element_type=jnp.float32) + add
    return lax.optimization_barrier((out * gelu_slope(pre)).astype(jnp.bfloat16))


def swap(x, axis):
    return lax.ppermute(x, axis, SWAP)


def solution(mesh):
    act_spec = P(("depth", "row"), "col")
    wgt_spec = P("row", "col")

    def grid_block(tok, up, down, grad):
        layer, col, row = lax.axis_index("depth"), lax.axis_index("col"), lax.axis_index("row")
        half = tok.shape[1]
        wide = up.shape[1]
        diag = row == col

        def join(a, b):
            return jnp.where(col == 0, jnp.concatenate([a, b], 1), jnp.concatenate([b, a], 1))

        q = wide // 2
        sub = lax.dynamic_slice(down, (row * q, layer * (half // 2)), (q, half // 2))
        oth = swap(lax.dynamic_slice(down, ((1 - row) * q, layer * (half // 2)), (q, half // 2)), "row")
        piece = jnp.where(diag, oth, sub)

        tok_1 = swap(tok, "col")
        tok_2 = swap(tok, "depth")
        grad_1 = swap(grad, "col")
        grad_2 = swap(grad, "depth")
        up_g = lax.all_gather(up, "row", axis=0, tiled=True)
        down_g = lax.all_gather(down, "row", axis=0, tiled=True)
        e = q // 2
        p1a, p1b = swap(piece[:e], "col"), swap(piece[e:], "col")
        p2a, p2b = swap(p1a, "depth"), swap(p1b, "depth")
        p1, p2 = jnp.concatenate([p1a, p1b], 0), jnp.concatenate([p2a, p2b], 0)
        tok_3 = swap(tok_1, "depth")
        grad_3 = swap(grad_1, "depth")
        down_a = lax.all_gather(p1, "row", axis=0, tiled=True)
        down_b = lax.all_gather(p2, "row", axis=0, tiled=True)
        down_c = lax.dynamic_slice_in_dim(down_g, col * wide, wide, 0)
        down_n = lax.dynamic_slice_in_dim(down_g, (1 - col) * wide, wide, 0)
        tok_h = join(tok, tok_1)
        tok_t = join(tok_2, tok_3)

        pre_h, act_h = forward(tok_h, up_g)
        pre_t, act_t = forward(tok_t, up_g)

        w = wide // PIECES
        cut = lambda x, j: x[:, j * w:(j + 1) * w]
        imp_h = [swap(cut(act_h, j), "col") for j in range(PIECES)]
        imp_t = [swap(imp_h[j], "depth") for j in range(PIECES)]

        first = lambda g: lax.dynamic_slice_in_dim(g, layer * (half // 2), half // 2, 1)
        second = lambda g: lax.dynamic_slice_in_dim(g, (1 - layer) * (half // 2), half // 2, 1)
        dh = dot(grad, down_c, "th,fh->tf")
        dh = dot(first(grad_1), down_a, "th,fh->tf", dh)
        du_h = backward(second(grad_1), down_b, dh, pre_h)
        part = dot(du_h, up_g, "tf,hf->th")
        away = swap(lax.dynamic_slice_in_dim(part, (1 - col) * half, half, 1), "col")
        grad_tok = (lax.dynamic_slice_in_dim(part, col * half, half, 1) + away).astype(jnp.bfloat16)
        dt = dot(grad_2, down_c, "th,fh->tf")
        dt = dot(first(grad_3), down_a, "th,fh->tf", dt)
        du_t = backward(second(grad_3), down_b, dt, pre_t)

        cols = lambda x, k: lax.dynamic_slice_in_dim(x, k * half, half, 1)
        tok_sh, tok_st = swap(cols(tok_h, 1 - row), "row"), swap(cols(tok_t, 1 - row), "row")
        du_sh, du_st = swap(du_h, "row"), swap(du_t, "row")
        up_sum = dot(cols(tok_h, row), du_h, "th,tf->hf")
        up_sum = dot(tok_sh, du_sh, "th,tf->hf", up_sum)
        up_sum = dot(cols(tok_t, row), du_t, "th,tf->hf", up_sum)
        up_sum = dot(tok_st, du_st, "th,tf->hf", up_sum)

        imp_ha = jnp.concatenate(imp_h, 1)
        imp_ta = jnp.concatenate(imp_t, 1)
        out = dot(act_h, down_c, "tf,fh->th")
        out = dot(imp_ha, down_n, "tf,fh->th", out).astype(jnp.bfloat16)

        grad_sh, grad_st = swap(grad, "row"), swap(grad_2, "row")
        oth_h = swap(jnp.where(diag, imp_ha, act_h), "row")
        oth_t = swap(jnp.where(diag, imp_ta, act_t), "row")
        down_sum = dot(jnp.where(diag, act_h, imp_ha), grad, "tf,th->fh")
        down_sum = dot(oth_h, grad_sh, "tf,th->fh", down_sum)
        down_sum = dot(jnp.where(diag, act_t, imp_ta), grad_2, "tf,th->fh", down_sum)
        down_sum = dot(oth_t, grad_st, "tf,th->fh", down_sum)
        return out, grad_tok, up_sum, down_sum

    return jax.shard_map(grid_block, mesh=mesh, in_specs=(act_spec, wgt_spec, wgt_spec, act_spec), out_specs=(act_spec, act_spec, wgt_spec, wgt_spec), check_vma=False)
```

time: 4960 us -> 2240 us (0.45)
  waiting for transfers between devices: 4330 us -> 1000 us
  matrix products: 491 us -> 1030 us
  other arithmetic: 6.05 us -> 82 us
    psum x2 -> x0, waiting for transfers between devices: 2760 us -> none  [the longest x1 1390 us: grid_block(): lax.psum(lax.psum_scatter(down_part, 'row', scatter_dimension=0, tiled=Tr...]
    ppermute x0 -> x28, waiting for transfers between devices: none -> 1000 us  [swap(): return lax.ppermute(x, axis, SWAP)]
    reduce_scatter x3 -> x0, waiting for transfers between devices: 920 us -> none  [the longest x1 730 us: grid_block(): lax.psum_scatter(act_part, 'col', scatter_dimension=1, tiled=True)]
    dot_general x6 -> x19, matrix products: 491 us -> 1030 us  [the longest x15 788 us: dot(): out = jnp.einsum(eq, a, b, preferred_element_type=jnp.float32)]
    all_gather x4, waiting for transfers between devices: 514 us -> 0.01 us  [the longest x1 0.01 us: grid_block(): down_g = lax.all_gather(down, 'row', axis=0, tiled=True)]
    unnamed x11 -> x4, waiting for transfers between devices: 133 us -> 1.39 us
    unnamed x2 -> x16, local copies, waits for them, and re-layouts: 105 us -> 27.7 us
    select_n x0 -> x5, other arithmetic: none -> 57.1 us  [the longest x2 19.2 us: join(): jnp.where(col == 0, jnp.concatenate([a, b], 1), jnp.concatenate([b, a], 1))]
  transfers between devices with their start and end apart: 10 -> 32, of which waited for: 9 -> 14; matrix products, arithmetic and copies ran while one was open for 9% -> 44% of each run, Pallas kernels for 0% -> 0%
where the time goes in v1:
time: 2240 us
  matrix products  1030 us (46%)
  waiting for transfers between devices  1000 us (45%)
  other arithmetic  82 us (4%)
  local copies, waits for them, and re-layouts  68.9 us (3%)
  starting transfers between devices  39.4 us (2%)
    ppermute x28, waiting for transfers between devices, swap(): return lax.ppermute(x, axis, SWAP)  1000 us
    dot_general x15, matrix products, dot(): out = jnp.einsum(eq, a, b, preferred_element_type=jnp.float32)  788 us
    dot_general x2, matrix products, forward(): pre = jnp.einsum('th,hf->tf', a, b, preferred_element_type=jnp.float32)  162 us
    dot_general x2, matrix products, backward(): jnp.einsum('th,fh->tf', a, b, preferred_element_type=jnp.float32) + add  81.1 us
  transfers between devices with their start and end apart: 32, of which 14 were waited for; matrix products, arithmetic and copies ran while one was open for 44% of the time, Pallas kernels for 0%

profile of v1, /device:TPU:0, one launch (start us, length us, event | category | flops | bytes accessed | tf_op | source)
XLA Modules:
  0.0 2237.6 jit_solution(14395152622495865750)
XLA Ops:
  46.3 90.2 %collective-permute-done.7 = bf16[2048,1024]{1,0:T(8,128)(2,1)} collective-permute-done((bf16[2048,1024]{1,0:T(8,128)(2,1)S(1)}, bf16[2048,1024]{1,0:T(8,128)(2,1)}, u32[]{:S(2)}, u32[]{:S(2)}) %collective-permute-start.7) | collective-permute-done | bytes 4194336 | tf_op jit(solution)/shard_map/ppermute | solution.py:37
  136.5 89.9 %collective-permute-done.9 = bf16[2048,1024]{1,0:T(8,128)(2,1)} collective-permute-done((bf16[2048,1024]{1,0:T(8,128)(2,1)S(1)}, bf16[2048,1024]{1,0:T(8,128)(2,1)}, u32[]{:S(2)}, u32[]{:S(2)}) %collective-permute-start.9) | collective-permute-done | bytes 4194336 | tf_op jit(solution)/shard_map/ppermute | solution.py:37
  241.4 87.4 %collective-permute-done = bf16[1024,2048]{1,0:T(8,128)(2,1)} collective-permute-done((bf16[1024,2048]{1,0:T(8,128)(2,1)}, bf16[1024,2048]{1,0:T(8,128)(2,1)}, u32[]{:S(2)}, u32[]{:S(2)}) %collective-permute-start) | collective-permute-done | bytes 4194336 | tf_op jit(solution)/shard_map/ppermute | solution.py:37
  347.5 71.2 %collective-permute-done.5 = bf16[1024,2048]{1,0:T(8,128)(2,1)} collective-permute-done((bf16[1024,2048]{1,0:T(8,128)(2,1)}, bf16[1024,2048]{1,0:T(8,128)(2,1)}, u32[]{:S(2)}, u32[]{:S(2)}) %collective-permute-start.5) | collective-permute-done | bytes 4194336 | tf_op jit(solution)/shard_map/ppermute | solution.py:37
  440.0 74.8 %collective-permute-done.8 = bf16[2048,1024]{1,0:T(8,128)(2,1)} collective-permute-done((bf16[2048,1024]{1,0:T(8,128)(2,1)}, bf16[2048,1024]{1,0:T(8,128)(2,1)}, u32[]{:S(2)}, u32[]{:S(2)}) %collective-permute-start.8) | collective-permute-done | bytes 4194336 | tf_op jit(solution)/shard_map/ppermute | solution.py:37
  514.8 89.9 %collective-permute-done.10 = bf16[2048,1024]{1,0:T(8,128)(2,1)} collective-permute-done((bf16[2048,1024]{1,0:T(8,128)(2,1)}, bf16[2048,1024]{1,0:T(8,128)(2,1)}, u32[]{:S(2)}, u32[]{:S(2)}) %collective-permute-start.10) | collective-permute-done | bytes 4194336 | tf_op jit(solution)/shard_map/ppermute | solution.py:37
  612.4 82.2 %collective-permute-done.16 = bf16[1024,2048]{1,0:T(8,128)(2,1)} collective-permute-done((bf16[1024,2048]{1,0:T(8,128)(2,1)}, bf16[1024,2048]{1,0:T(8,128)(2,1)}, u32[]{:S(2)}, u32[]{:S(2)}) %collective-permute-start.16) | collective-permute-done | bytes 4194336 | tf_op jit(solution)/shard_map/ppermute | solution.py:37
  694.6 41.8 %fusion.23 = f32[1024,8192]{1,0:T(8,128)} fusion(bf16[1024,2048]{1,0:T(8,128)(2,1)} %collective-permute-done.16, bf16[16384,2048]{1,0:T(8,128)(2,1)} %all-gather.7.cloned.1.call-done, s32[]{:T(128)S(6)} %select_n.79), kind=kOutput, calls=%fused_computation.33 | convolution fusion | flops 34359738368 | bytes 71303168 | tf_op jit(solution)/shard_map/th,fh->tf/dot_general | solution.py:22
  736.4 45.2 %collective-permute-done.15 = bf16[1024,2048]{1,0:T(8,128)(2,1)} collective-permute-done((bf16[1024,2048]{1,0:T(8,128)(2,1)}, bf16[1024,2048]{1,0:T(8,128)(2,1)}, u32[]{:S(2)}, u32[]{:S(2)}) %collective-permute-start.15) | collective-permute-done | bytes 4194336 | tf_op jit(solution)/shard_map/ppermute | solution.py:37
  781.6 32.9 %convolution_add_fusion.6 = f32[1024,8192]{1,0:T(8,128)} fusion(f32[1024,8192]{1,0:T(8,128)} %fusion.23, bf16[8192,1024]{1,0:T(8,128)(2,1)} %all-gather.11.cloned.1.call-done, bf16[1024,2048]{1,0:T(8,128)(2,1)} %collective-permute-done.15, s32[]{:T(128)S(6)} %select_n.83), kind=kOutput, calls=%fused_computation.30 | convolution fusion | flops 17188257792 | bytes 85983232 | tf_op jit(solution)/shard_map/th,fh->tf/dot_general | solution.py:22
  814.5 42.0 %fusion.20 = f32[1024,8192]{1,0:T(8,128)} fusion(bf16[1024,2048]{1,0:T(8,128)(2,1)} %param.7, bf16[16384,2048]{1,0:T(8,128)(2,1)} %all-gather.7.cloned.1.call-done, s32[]{:T(128)S(6)} %select_n.79), kind=kOutput, calls=%fused_computation.32 | convolution fusion | flops 34359738368 | bytes 71303168 | tf_op jit(solution)/shard_map/th,fh->tf/dot_general | solution.py:22
  856.4 33.0 %convolution_add_fusion.7 = f32[1024,8192]{1,0:T(8,128)} fusion(f32[1024,8192]{1,0:T(8,128)} %fusion.20, bf16[8192,1024]{1,0:T(8,128)(2,1)} %all-gather.11.cloned.1.call-done, bf16[1024,2048]{1,0:T(8,128)(2,1)} %collective-permute-done.5, s32[]{:T(128)S(6)} %select_n.83), kind=kOutput, calls=%fused_computation.31 | convolution fusion | flops 17188257792 | bytes 85983232 | tf_op jit(solution)/shard_map/th,fh->tf/dot_general | solution.py:22
  889.5 81.3 %multiply_convert_fusion.1 = (bf16[1024,8192]{1,0:T(8,128)(2,1)}, f32[1024,8192]{1,0:T(8,128)}) fusion(bf16[1024,4096]{1,0:T(8,128)(2,1)} %copy-done.2, bf16[4096,8192]{1,0:T(8,128)(2,1)} %all-gather.5.cloned.1.call-done), kind=kOutput, calls=%fused_computation.23 | convolution fusion | flops 68761419776 | bytes 125829120 | tf_op jit(solution)/shard_map/th,hf->tf/dot_general | solution.py:27
  970.7 40.6 %fusion.5 = bf16[1024,8192]{1,0:T(8,128)(2,1)} fusion(f32[1024,8192]{1,0:T(8,128)} %get-tuple-element.9, f32[1024,8192]{1,0:T(8,128)} %convolution_add_fusion.7, bf16[8192,1024]{1,0:T(8,128)(2,1)} %all-gather.9.cloned.1.call-done, bf16[1024,2048]{1,0:T(8,128)(2,1)} %collective-permute-done.5, s32[]{:T(128)S(6)} %select_n.80), kind=kOutput, calls=%fused_computation.13 | convolution fusion | flops 17272143872 | bytes 102760448 | tf_op jit(solution)/shard_map/th,fh->tf/dot_general | solution.py:32
  1011.3 81.0 %multiply_convert_fusion = (bf16[1024,8192]{1,0:T(8,128)(2,1)}, f32[1024,8192]{1,0:T(8,128)}) fusion(bf16[1024,4096]{1,0:T(8,128)(2,1)} %copy-done, bf16[4096,8192]{1,0:T(8,128)(2,1)} %all-gather.5.cloned.1.call-done), kind=kOutput, calls=%fused_computation.20 | convolution fusion | flops 68761419776 | bytes 125829120 | tf_op jit(solution)/shard_map/th,hf->tf/dot_general | solution.py:27
  1108.9 45.6 %fusion.31 = f32[2048,8192]{1,0:T(8,128)} fusion(bf16[1024,8192]{1,0:T(8,128)(2,1)} %fusion.5, bf16[1024,4096]{1,0:T(8,128)(2,1)} %copy-done.2, s32[]{:T(128)S(6)} %select_n.90), kind=kOutput, calls=%fused_computation.47 | convolution fusion | flops 34359738368 | bytes 88080384 | tf_op jit(solution)/shard_map/th,tf->hf/dot_general | solution.py:22
  1154.6 43.5 %fusion.18 = f32[1024,2048]{1,0:T(8,128)} fusion(bf16[1024,8192]{1,0:T(8,128)(2,1)} %get-tuple-element.8, bf16[16384,2048]{1,0:T(8,128)(2,1)} %all-gather.7.cloned.1.call-done, s32[]{:T(128)S(6)} %select_n.79), kind=kOutput, calls=%fused_computation.28 | convolution fusion | flops 34359738368 | bytes 58720260 | tf_op jit(solution)/shard_map/tf,fh->th/dot_general | solution.py:22
  1198.1 80.7 %fusion.53 = f32[1024,4096]{1,0:T(8,128)} fusion(bf16[1024,8192]{1,0:T(8,128)(2,1)} %fusion.5, bf16[4096,8192]{1,0:T(8,128)(2,1)} %all-gather.5.cloned.1.call-done), kind=kOutput, calls=%fused_computation.78 | convolution fusion | flops 68719476736 | bytes 100663296 | tf_op jit(solution)/shard_map/tf,hf->th/dot_general | solution.py:22
  1278.8 40.6 %fusion.11 = bf16[1024,8192]{1,0:T(8,128)(2,1)} fusion(f32[1024,8192]{1,0:T(8,128)} %get-tuple-element.10, f32[1024,8192]{1,0:T(8,128)} %convolution_add_fusion.6, bf16[8192,1024]{1,0:T(8,128)(2,1)} %all-gather.9.cloned.1.call-done, bf16[1024,2048]{1,0:T(8,128)(2,1)} %collective-permute-done.15, s32[]{:T(128)S(6)} %select_n.80), kind=kOutput, calls=%fused_computation.19 | convolution fusion | flops 17272143872 | bytes 102760448 | tf_op jit(solution)/shard_map/th,fh->tf/dot_general | solution.py:32
  1327.1 51.3 %collective-permute-done.2 = bf16[1024,2048]{1,0:T(8,128)(2,1)} collective-permute-done((bf16[1024,2048]{1,0:T(8,128)(2,1)}, bf16[1024,2048]{1,0:T(8,128)(2,1)}, u32[]{:S(2)}, u32[]{:S(2)}) %collective-permute-start.2) | collective-permute-done | bytes 4194336 | tf_op jit(solution)/shard_map/ppermute | solution.py:37
  1380.1 88.2 %collective-permute-done.1 = bf16[1024,2048]{1,0:T(8,128)(2,1)} collective-permute-done((bf16[1024,2048]{1,0:T(8,128)(2,1)}, bf16[1024,2048]{1,0:T(8,128)(2,1)}, u32[]{:S(2)}, u32[]{:S(2)}) %collective-permute-start.1) | collective-permute-done | bytes 4194336 | tf_op jit(solution)/shard_map/ppermute | solution.py:37
  1489.5 45.2 %fusion.34 = bf16[1024,2048]{1,0:T(8,128)(2,1)} fusion(f32[1024,2048]{1,0:T(8,128)} %fusion.18, bf16[1024,8192]{1,0:T(8,128)(2,1)} %constant_dynamic-update-slice_fusion, bf16[16384,2048]{1,0:T(8,128)(2,1)} %all-gather.7.cloned.1.call-done, s32[]{:T(128)S(6)} %select_n.78), kind=kOutput, calls=%fused_computation.50 | convolution fusion | flops 34363932672 | bytes 62914564 | tf_op jit(solution)/shard_map/tf,fh->th/dot_general | solution.py:22
  1534.7 46.0 %fusion.26 = f32[8192,2048]{1,0:T(8,128)} fusion(bf16[1024,2048]{1,0:T(8,128)(2,1)} %param.7, bf16[1024,8192]{1,0:T(8,128)(2,1)} %get-tuple-element.8, bf16[1024,8192]{1,0:T(8,128)(2,1)} %constant_dynamic-update-slice_fusion, pred[]{:T(512)S(6)} %eq.8), kind=kOutput, calls=%fused_computation.34 | convolution fusion | flops 34368126976 | bytes 104857600 | tf_op jit(solution)/shard_map/tf,th->fh/dot_general | solution.py:22
  1582.1 63.5 %collective-permute-done.11 = f32[1024,2048]{1,0:T(8,128)} collective-permute-done((f32[1024,2048]{1,0:T(8,128)}, f32[1024,2048]{1,0:T(8,128)}, u32[]{:S(2)}, u32[]{:S(2)}) %collective-permute-start.11) | collective-permute-done | bytes 8388640 | tf_op jit(solution)/shard_map/ppermute | solution.py:37
  1647.1 14.5 broadcast_select_fusion
  1676.6 149.5 %collective-permute-done.22 = bf16[1024,2048]{1,0:T(8,128)(2,1)} collective-permute-done((bf16[1024,2048]{1,0:T(8,128)(2,1)}, bf16[1024,2048]{1,0:T(8,128)(2,1)}, u32[]{:S(2)}, u32[]{:S(2)}) %collective-permute-start.22) | collective-permute-done | bytes 4194336 | tf_op jit(solution)/shard_map/ppermute | solution.py:37
  1852.9 63.5 %convolution_add_fusion.3 = f32[2048,8192]{1,0:T(8,128)} fusion(f32[2048,8192]{1,0:T(8,128)} %fusion.31, bf16[1024,2048]{1,0:T(8,128)(2,1)} %copy-done.3, bf16[1024,8192]{1,0:T(8,128)(2,1)} %collective-permute-done.19), kind=kOutput, calls=%fused_computation.5 | convolution fusion | flops 34376515584 | bytes 155189248 | tf_op jit(solution)/shard_map/th,tf->hf/dot_general | solution.py:22
  1916.4 63.7 %convolution_add_fusion.4 = f32[2048,8192]{1,0:T(8,128)} fusion(f32[2048,8192]{1,0:T(8,128)} %convolution_add_fusion.3, bf16[1024,8192]{1,0:T(8,128)(2,1)} %fusion.11, bf16[1024,4096]{1,0:T(8,128)(2,1)} %copy-done, s32[]{:T(128)S(6)} %select_n.90), kind=kOutput, calls=%fused_computation.6 | convolution fusion | flops 34376515584 | bytes 155189248 | tf_op jit(solution)/shard_map/th,tf->hf/dot_general | solution.py:22
  1980.6 63.5 %convolution_add_fusion.5 = f32[2048,8192]{1,0:T(8,128)} fusion(f32[2048,8192]{1,0:T(8,128)} %convolution_add_fusion.4, bf16[1024,2048]{1,0:T(8,128)(2,1)} %collective-permute-done.14, bf16[1024,8192]{1,0:T(8,128)(2,1)} %collective-permute-done.17), kind=kOutput, calls=%fused_computation.7 | convolution fusion | flops 34376515584 | bytes 155189248 | tf_op jit(solution)/shard_map/th,tf->hf/dot_general | solution.py:22
  2044.1 62.2 %convolution_add_fusion = f32[8192,2048]{1,0:T(8,128)} fusion(f32[8192,2048]{1,0:T(8,128)} %fusion.26, bf16[1024,8192]{1,0:T(8,128)(2,1)} %collective-permute-done.26, bf16[1024,2048]{1,0:T(8,128)(2,1)} %collective-permute-done.27), kind=kOutput, calls=%fused_computation.2 | convolution fusion | flops 34376515584 | bytes 155189248 | tf_op jit(solution)/shard_map/tf,th->fh/dot_general | solution.py:22
  2106.3 62.3 %convolution_add_fusion.1 = f32[8192,2048]{1,0:T(8,128)} fusion(f32[8192,2048]{1,0:T(8,128)} %convolution_add_fusion, bf16[1024,2048]{1,0:T(8,128)(2,1)} %collective-permute-done.16, bf16[1024,8192]{1,0:T(8,128)(2,1)} %get-tuple-element.11, bf16[1024,8192]{1,0:T(8,128)(2,1)} %copy-done.1, pred[]{:T(512)S(6)} %eq.8), kind=kOutput, calls=%fused_computation.3 | convolution fusion | flops 34384904192 | bytes 171966464 | tf_op jit(solution)/shard_map/tf,th->fh/dot_general | solution.py:22
  2168.6 62.2 %convolution_add_fusion.2 = f32[8192,2048]{1,0:T(8,128)} fusion(f32[8192,2048]{1,0:T(8,128)} %convolution_add_fusion.1, bf16[1024,8192]{1,0:T(8,128)(2,1)} %collective-permute-done.24, bf16[1024,2048]{1,0:T(8,128)(2,1)} %collective-permute-done.25), kind=kOutput, calls=%fused_computation.4 | convolution fusion | flops 34376515584 | bytes 155189248 | tf_op jit(solution)/shard_map/tf,th->fh/dot_general | solution.py:22
  (87 shorter events, 194.1 us)
Async XLA Ops:
  7.2 687.4 %all-gather.7.cloned.1.call-start = ((), (), s32[]{:S(2)}) async-start(), calls=%async_computation.1 | async-start | bytes 100663296 | tf_op jit(solution)/shard_map/all_gather | solution.py:63
  7.9 773.7 %all-gather.11.cloned.1.call-start = ((), (), s32[]{:S(2)}) async-start(), calls=%async_computation.3 | async-start | bytes 25165824 | tf_op jit(solution)/shard_map/all_gather | solution.py:70
  15.8 14.3 collective-permute-start.6
  44.2 92.3 %collective-permute-start.7 = (bf16[2048,1024]{1,0:T(8,128)(2,1)S(1)}, bf16[2048,1024]{1,0:T(8,128)(2,1)}, u32[]{:S(2)}, u32[]{:S(2)}) collective-permute-start(bf16[2048,1024]{1,0:T(8,128)(2,1)S(1)} %get-tuple-element.16), channel_id=1, source_target_pairs={{0,2},{2,0},{1,3},{3,1},{4,6},{6,4},{5,7},{7,5}} | collective-permute-start | bytes 12582920 | tf_op jit(solution)/shard_map/ppermute | solution.py:37
  44.3 182.1 %collective-permute-start.9 = (bf16[2048,1024]{1,0:T(8,128)(2,1)S(1)}, bf16[2048,1024]{1,0:T(8,128)(2,1)}, u32[]{:S(2)}, u32[]{:S(2)}) collective-permute-start(bf16[2048,1024]{1,0:T(8,128)(2,1)S(1)} %get-tuple-element.17), channel_id=1, source_target_pairs={{0,2},{2,0},{1,3},{3,1},{4,6},{6,4},{5,7},{7,5}} | collective-permute-start | bytes 12582920 | tf_op jit(solution)/shard_map/ppermute | solution.py:37
  234.3 655.2 %all-gather.5.cloned.1.call-start = ((), (), s32[]{:S(2)}) async-start(), calls=%async_computation | async-start | bytes 100663296 | tf_op jit(solution)/shard_map/all_gather | solution.py:62
  235.0 735.7 %all-gather.9.cloned.1.call-start = ((), (), s32[]{:S(2)}) async-start(), calls=%async_computation.2 | async-start | bytes 25165824 | tf_op jit(solution)/shard_map/all_gather | solution.py:71
  235.2 93.6 %collective-permute-start = (bf16[1024,2048]{1,0:T(8,128)(2,1)}, bf16[1024,2048]{1,0:T(8,128)(2,1)}, u32[]{:S(2)}, u32[]{:S(2)}) collective-permute-start(bf16[1024,2048]{1,0:T(8,128)(2,1)} %param.4), channel_id=1, source_target_pairs={{0,2},{2,0},{1,3},{3,1},{4,6},{6,4},{5,7},{7,5}} | collective-permute-start | bytes 12582920 | tf_op jit(solution)/shard_map/ppermute | solution.py:37
  235.3 100.0 %collective-permute-start.12 = (bf16[1024,2048]{1,0:T(8,128)(2,1)}, bf16[1024,2048]{1,0:T(8,128)(2,1)}, u32[]{:S(2)}, u32[]{:S(2)}) collective-permute-start(bf16[1024,2048]{1,0:T(8,128)(2,1)} %param.4), channel_id=1, source_target_pairs={{0,4},{4,0},{1,5},{5,1},{2,6},{6,2},{3,7},{7,3}} | collective-permute-start | bytes 12582920 | tf_op jit(solution)/shard_map/ppermute | solution.py:37
  239.8 178.9 %collective-permute-start.5 = (bf16[1024,2048]{1,0:T(8,128)(2,1)}, bf16[1024,2048]{1,0:T(8,128)(2,1)}, u32[]{:S(2)}, u32[]{:S(2)}) collective-permute-start(bf16[1024,2048]{1,0:T(8,128)(2,1)} %param.7), channel_id=1, source_target_pairs={{0,2},{2,0},{1,3},{3,1},{4,6},{6,4},{5,7},{7,5}} | collective-permute-start | bytes 12582920 | tf_op jit(solution)/shard_map/ppermute | solution.py:37
  328.8 96.1 %collective-permute-start.13 = (bf16[1024,2048]{1,0:T(8,128)(2,1)}, bf16[1024,2048]{1,0:T(8,128)(2,1)}, u32[]{:S(2)}, u32[]{:S(2)}) collective-permute-start(bf16[1024,2048]{1,0:T(8,128)(2,1)} %collective-permute-done), channel_id=1, source_target_pairs={{0,4},{4,0},{1,5},{5,1},{2,6},{6,2},{3,7},{7,3}} | collective-permute-start | bytes 12582920 | tf_op jit(solution)/shard_map/ppermute | solution.py:37
  333.2 181.6 %collective-permute-start.8 = (bf16[2048,1024]{1,0:T(8,128)(2,1)}, bf16[2048,1024]{1,0:T(8,128)(2,1)}, u32[]{:S(2)}, u32[]{:S(2)}) collective-permute-start(bf16[2048,1024]{1,0:T(8,128)(2,1)} %collective-permute-done.7), channel_id=1, source_target_pairs={{0,4},{4,0},{1,5},{5,1},{2,6},{6,2},{3,7},{7,3}} | collective-permute-start | bytes 12582920 | tf_op jit(solution)/shard_map/ppermute | solution.py:37
  333.2 271.5 %collective-permute-start.10 = (bf16[2048,1024]{1,0:T(8,128)(2,1)}, bf16[2048,1024]{1,0:T(8,128)(2,1)}, u32[]{:S(2)}, u32[]{:S(2)}) collective-permute-start(bf16[2048,1024]{1,0:T(8,128)(2,1)} %collective-permute-done.9), channel_id=1, source_target_pairs={{0,4},{4,0},{1,5},{5,1},{2,6},{6,2},{3,7},{7,3}} | collective-permute-start | bytes 12582920 | tf_op jit(solution)/shard_map/ppermute | solution.py:37
  335.2 359.4 %collective-permute-start.16 = (bf16[1024,2048]{1,0:T(8,128)(2,1)}, bf16[1024,2048]{1,0:T(8,128)(2,1)}, u32[]{:S(2)}, u32[]{:S(2)}) collective-permute-start(bf16[1024,2048]{1,0:T(8,128)(2,1)} %param.7), channel_id=1, source_target_pairs={{0,4},{4,0},{1,5},{5,1},{2,6},{6,2},{3,7},{7,3}} | collective-permute-start | bytes 12582920 | tf_op jit(solution)/shard_map/ppermute | solution.py:37
  418.7 362.9 %collective-permute-start.15 = (bf16[1024,2048]{1,0:T(8,128)(2,1)}, bf16[1024,2048]{1,0:T(8,128)(2,1)}, u32[]{:S(2)}, u32[]{:S(2)}) collective-permute-start(bf16[1024,2048]{1,0:T(8,128)(2,1)} %collective-permute-done.5), channel_id=1, source_target_pairs={{0,4},{4,0},{1,5},{5,1},{2,6},{6,2},{3,7},{7,3}} | collective-permute-start | bytes 12582920 | tf_op jit(solution)/shard_map/ppermute | solution.py:37
  1104.9 379.8 %collective-permute-start.4 = (bf16[1024,2048]{1,0:T(8,128)(2,1)}, bf16[1024,2048]{1,0:T(8,128)(2,1)}, u32[]{:S(2)}, u32[]{:S(2)}) collective-permute-start(bf16[1024,2048]{1,0:T(8,128)(2,1)} %get-tuple-element.12), channel_id=1, source_target_pairs={{0,2},{2,0},{1,3},{3,1},{4,6},{6,4},{5,7},{7,5}} | collective-permute-start | bytes 12582920 | tf_op jit(solution)/shard_map/ppermute | solution.py:37
  1106.6 372.7 %collective-permute-start.3 = (bf16[1024,2048]{1,0:T(8,128)(2,1)}, bf16[1024,2048]{1,0:T(8,128)(2,1)}, u32[]{:S(2)}, u32[]{:S(2)}) collective-permute-start(bf16[1024,2048]{1,0:T(8,128)(2,1)} %get-tuple-element.13), channel_id=1, source_target_pairs={{0,2},{2,0},{1,3},{3,1},{4,6},{6,4},{5,7},{7,5}} | collective-permute-start | bytes 12582920 | tf_op jit(solution)/shard_map/ppermute | solution.py:37
  1106.9 271.5 %collective-permute-start.2 = (bf16[1024,2048]{1,0:T(8,128)(2,1)}, bf16[1024,2048]{1,0:T(8,128)(2,1)}, u32[]{:S(2)}, u32[]{:S(2)}) collective-permute-start(bf16[1024,2048]{1,0:T(8,128)(2,1)} %get-tuple-element.14), channel_id=1, source_target_pairs={{0,2},{2,0},{1,3},{3,1},{4,6},{6,4},{5,7},{7,5}} | collective-permute-start | bytes 12582920 | tf_op jit(solution)/shard_map/ppermute | solution.py:37
  1108.6 359.6 %collective-permute-start.1 = (bf16[1024,2048]{1,0:T(8,128)(2,1)}, bf16[1024,2048]{1,0:T(8,128)(2,1)}, u32[]{:S(2)}, u32[]{:S(2)}) collective-permute-start(bf16[1024,2048]{1,0:T(8,128)(2,1)} %get-tuple-element.15), channel_id=1, source_target_pairs={{0,2},{2,0},{1,3},{3,1},{4,6},{6,4},{5,7},{7,5}} | collective-permute-start | bytes 12582920 | tf_op jit(solution)/shard_map/ppermute | solution.py:37
  1108.9 744.0 %collective-permute-start.19 = (bf16[1024,8192]{1,0:T(8,128)(2,1)}, bf16[1024,8192]{1,0:T(8,128)(2,1)}, u32[]{:S(2)}, u32[]{:S(2)}) collective-permute-start(bf16[1024,8192]{1,0:T(8,128)(2,1)} %fusion.5), channel_id=1, source_target_pairs={{0,1},{1,0},{2,3},{3,2},{4,5},{5,4},{6,7},{7,6}} | collective-permute-start | bytes 50331656 | tf_op jit(solution)/shard_map/ppermute | solution.py:37
  1378.4 267.3 %collective-permute-start.11 = (f32[1024,2048]{1,0:T(8,128)}, f32[1024,2048]{1,0:T(8,128)}, u32[]{:S(2)}, u32[]{:S(2)}) collective-permute-start(f32[1024,2048]{1,0:T(8,128)} %constant_dynamic-slice_fusion.2), channel_id=1, source_target_pairs={{0,2},{2,0},{1,3},{3,1},{4,6},{6,4},{5,7},{7,5}} | collective-permute-start | bytes 25165832 | tf_op jit(solution)/shard_map/ppermute | solution.py:37
  1468.3 205.3 %collective-permute-start.21 = (bf16[1024,2048]{1,0:T(8,128)(2,1)}, bf16[1024,2048]{1,0:T(8,128)(2,1)}, u32[]{:S(2)}, u32[]{:S(2)}) collective-permute-start(bf16[1024,2048]{1,0:T(8,128)(2,1)} %collective-permute-done.2), channel_id=1, source_target_pairs={{0,4},{4,0},{1,5},{5,1},{2,6},{6,2},{3,7},{7,3}} | collective-permute-start | bytes 12582920 | tf_op jit(solution)/shard_map/ppermute | solution.py:37
  1479.3 191.8 %collective-permute-start.20 = (bf16[1024,2048]{1,0:T(8,128)(2,1)}, bf16[1024,2048]{1,0:T(8,128)(2,1)}, u32[]{:S(2)}, u32[]{:S(2)}) collective-permute-start(bf16[1024,2048]{1,0:T(8,128)(2,1)} %collective-permute-done.1), channel_id=1, source_target_pairs={{0,4},{4,0},{1,5},{5,1},{2,6},{6,2},{3,7},{7,3}} | collective-permute-start | bytes 12582920 | tf_op jit(solution)/shard_map/ppermute | solution.py:37
  1580.7 247.9 %collective-permute-start.23 = (bf16[1024,2048]{1,0:T(8,128)(2,1)}, bf16[1024,2048]{1,0:T(8,128)(2,1)}, u32[]{:S(2)}, u32[]{:S(2)}) collective-permute-start(bf16[1024,2048]{1,0:T(8,128)(2,1)} %collective-permute-done.4), channel_id=1, source_target_pairs={{0,4},{4,0},{1,5},{5,1},{2,6},{6,2},{3,7},{7,3}} | collective-permute-start | bytes 12582920 | tf_op jit(solution)/shard_map/ppermute | solution.py:37
  1645.7 180.4 %collective-permute-start.22 = (bf16[1024,2048]{1,0:T(8,128)(2,1)}, bf16[1024,2048]{1,0:T(8,128)(2,1)}, u32[]{:S(2)}, u32[]{:S(2)}) collective-permute-start(bf16[1024,2048]{1,0:T(8,128)(2,1)} %collective-permute-done.3), channel_id=1, source_target_pairs={{0,4},{4,0},{1,5},{5,1},{2,6},{6,2},{3,7},{7,3}} | collective-permute-start | bytes 12582920 | tf_op jit(solution)/shard_map/ppermute | solution.py:37
  1671.1 171.4 %collective-permute-start.18 = (bf16[1024,2048]{1,0:T(8,128)(2,1)S(1)}, bf16[1024,2048]{1,0:T(8,128)(2,1)S(1)}, u32[]{:S(2)}, u32[]{:S(2)}) collective-permute-start(bf16[1024,2048]{1,0:T(8,128)(2,1)S(1)} %copy-done.4), channel_id=1, source_target_pairs={{0,1},{1,0},{2,3},{3,2},{4,5},{5,4},{6,7},{7,6}} | collective-permute-start | bytes 12582920 | tf_op jit(solution)/shard_map/ppermute | solution.py:37
  1673.6 370.5 %collective-permute-start.27 = (bf16[1024,2048]{1,0:T(8,128)(2,1)}, bf16[1024,2048]{1,0:T(8,128)(2,1)}, u32[]{:S(2)}, u32[]{:S(2)}) collective-permute-start(bf16[1024,2048]{1,0:T(8,128)(2,1)} %param.7), channel_id=1, source_target_pairs={{0,1},{1,0},{2,3},{3,2},{4,5},{5,4},{6,7},{7,6}} | collective-permute-start | bytes 12582920 | tf_op jit(solution)/shard_map/ppermute | solution.py:37
  1826.1 342.5 %collective-permute-start.25 = (bf16[1024,2048]{1,0:T(8,128)(2,1)}, bf16[1024,2048]{1,0:T(8,128)(2,1)}, u32[]{:S(2)}, u32[]{:S(2)}) collective-permute-start(bf16[1024,2048]{1,0:T(8,128)(2,1)} %collective-permute-done.16), channel_id=1, source_target_pairs={{0,1},{1,0},{2,3},{3,2},{4,5},{5,4},{6,7},{7,6}} | collective-permute-start | bytes 12582920 | tf_op jit(solution)/shard_map/ppermute | solution.py:37
  1828.6 151.5 %collective-permute-start.14 = (bf16[1024,2048]{1,0:T(8,128)(2,1)}, bf16[1024,2048]{1,0:T(8,128)(2,1)}, u32[]{:S(2)}, u32[]{:S(2)}) collective-permute-start(bf16[1024,2048]{1,0:T(8,128)(2,1)} %constant_dynamic-slice_fusion.1), channel_id=1, source_target_pairs={{0,1},{1,0},{2,3},{3,2},{4,5},{5,4},{6,7},{7,6}} | collective-permute-start | bytes 12582920 | tf_op jit(solution)/shard_map/ppermute | solution.py:37
  1844.5 136.2 %collective-permute-start.17 = (bf16[1024,8192]{1,0:T(8,128)(2,1)}, bf16[1024,8192]{1,0:T(8,128)(2,1)}, u32[]{:S(2)}, u32[]{:S(2)}) collective-permute-start(bf16[1024,8192]{1,0:T(8,128)(2,1)} %fusion.11), channel_id=1, source_target_pairs={{0,1},{1,0},{2,3},{3,2},{4,5},{5,4},{6,7},{7,6}} | collective-permute-start | bytes 50331656 | tf_op jit(solution)/shard_map/ppermute | solution.py:37
  1852.9 191.2 %collective-permute-start.26 = (bf16[1024,8192]{1,0:T(8,128)(2,1)}, bf16[1024,8192]{1,0:T(8,128)(2,1)}, u32[]{:S(2)}, u32[]{:S(2)}) collective-permute-start(bf16[1024,8192]{1,0:T(8,128)(2,1)} %broadcast_select_fusion), channel_id=1, source_target_pairs={{0,1},{1,0},{2,3},{3,2},{4,5},{5,4},{6,7},{7,6}} | collective-permute-start | bytes 50331656 | tf_op jit(solution)/shard_map/ppermute | solution.py:37
  1980.1 188.5 %collective-permute-start.24 = (bf16[1024,8192]{1,0:T(8,128)(2,1)}, bf16[1024,8192]{1,0:T(8,128)(2,1)}, u32[]{:S(2)}, u32[]{:S(2)}) collective-permute-start(bf16[1024,8192]{1,0:T(8,128)(2,1)} %broadcast_select_fusion.1), channel_id=1, source_target_pairs={{0,1},{1,0},{2,3},{3,2},{4,5},{5,4},{6,7},{7,6}} | collective-permute-start | bytes 50331656 | tf_op jit(solution)/shard_map/ppermute | solution.py:37
  (5 other events, 101.8 us)
Sparse Core Ops, SparseCore 0:
  9.5 94.8 all-gather.6
  234.4 29.9 all-gather.10
  265.9 93.2 all-gather.4
  612.5 27.8 all-gather.8

commit v2 on v1

v2 whole, which is shorter than its diff:
```python
import functools
import math
import jax
import jax.numpy as jnp
from jax import lax
from jax.experimental import pallas as pl
from jax.experimental.pallas import tpu as pltpu
from jax.sharding import PartitionSpec as P

INV_ROOT_TWO = 1.0 / math.sqrt(2.0)
INV_ROOT_TAU = 1.0 / math.sqrt(2.0 * math.pi)
SWAP = [(0, 1), (1, 0)]
PIECES = 4
PARTS = 2


ANY = pl.BlockSpec(memory_space=pl.ANY)
F32, BF16 = jnp.float32, jnp.bfloat16

TN = (((0,), (0,)), ((), ()))
NN = (((1,), (0,)), ((), ()))
NT = (((1,), (1,)), ((), ()))


def cost(m, n, k):
    return pl.CostEstimate(flops=2 * m * n * k, bytes_accessed=2 * (m * k + n * k) + 4 * m * n, transcendentals=0)


def up_kernel(x0, x1, x2, x3, d0, d1, d2, d3, out, lhs, sem):
    depth = x0.shape[1]
    copies = [pltpu.make_async_copy(x, lhs.at[:, pl.ds(k * depth, depth)], sem.at[k]) for k, x in enumerate((x0, x1, x2, x3))]

    @pl.when(pl.program_id(0) == 0)
    def _():
        for c in copies:
            c.start()
        for c in copies:
            c.wait()

    total = None
    for k, d in enumerate((d0, d1, d2, d3)):
        part = lax.dot_general(lhs[:, k * depth:(k + 1) * depth], d[...], NN, preferred_element_type=jnp.float32)
        total = part if total is None else total + part
    out[...] = total


def up_grad(xs, ds, bn=512):
    m, depth = xs[0].shape
    n = ds[0].shape[1]
    return pl.pallas_call(
        up_kernel,
        grid=(n // bn,),
        out_shape=jax.ShapeDtypeStruct((m, n), jnp.float32),
        in_specs=[pl.BlockSpec(memory_space=pl.ANY)] * 4 + [pl.BlockSpec((depth, bn), lambda i: (0, i))] * 4,
        out_specs=pl.BlockSpec((m, bn), lambda i: (0, i)),
        scratch_shapes=[pltpu.VMEM((m, 4 * depth), jnp.bfloat16), pltpu.SemaphoreType.DMA((4,))],
        compiler_params=params(),
        cost_estimate=cost(m, n, 4 * depth),
        name="up_grad",
    )(*xs, *ds)


def down_kernel(pieces, *refs):
    act_h, act_t, imp_h, imp_t, oth_h, oth_t = [refs[n * pieces:(n + 1) * pieces] for n in range(6)]
    g = refs[6 * pieces:6 * pieces + 4]
    out, lhs, rhs, sem, rsem = refs[-5:]
    i, n = pl.program_id(0), pl.num_programs(0)
    bm = out.shape[0]
    depth = g[0].shape[0]
    per = imp_h[0].shape[1] // bm
    diag = lax.axis_index("row") == lax.axis_index("col")

    def put(src, col, slot, k):
        return pltpu.make_async_copy(src.at[:, pl.ds(pl.multiple_of(col * bm, bm), bm)], lhs.at[slot, pl.ds(k * depth, depth)], sem.at[slot, k])

    def fetch(t):
        slot = lax.rem(t, 2)
        for j in range(pieces):
            @pl.when(t // per == j)
            def _():
                put(oth_h[j], lax.rem(t, per), slot, 1).start()
                put(oth_t[j], lax.rem(t, per), slot, 3).start()

            @pl.when(jnp.logical_and(t // per == j, diag))
            def _():
                put(act_h[j], lax.rem(t, per), slot, 0).start()
                put(act_t[j], lax.rem(t, per), slot, 2).start()

            @pl.when(jnp.logical_and(t // per == j, jnp.logical_not(diag)))
            def _():
                put(imp_h[j], lax.rem(t, per), slot, 0).start()
                put(imp_t[j], lax.rem(t, per), slot, 2).start()

    @pl.when(i == 0)
    def _():
        fetch(i)
        loads = [pltpu.make_async_copy(x, rhs.at[pl.ds(k * depth, depth)], rsem.at[k]) for k, x in enumerate(g)]
        for c in loads:
            c.start()
        for c in loads:
            c.wait()

    @pl.when(i + 1 < n)
    def _():
        fetch(i + 1)

    slot = lax.rem(i, 2)
    for k in range(4):
        put(act_h[0], 0, slot, k).wait()
    out[...] = lax.dot_general(lhs[slot], rhs[...], TN, preferred_element_type=jnp.float32)


def down_grad(act_h, act_t, imp_h, imp_t, oth_h, oth_t, gs, part, before, bm=512):
    pieces = len(imp_h)
    depth, n = gs[0].shape
    m = pieces * act_h[0].shape[1]
    ops = [*act_h, *act_t, *imp_h, *imp_t, *oth_h, *oth_t, *gs]
    aliases = {}
    if before is not None:
        aliases = {len(ops): 0}
        ops.append(before)
    steps = m // bm
    return pl.pallas_call(
        functools.partial(down_kernel, pieces),
        grid=(steps,),
        out_shape=jax.ShapeDtypeStruct((m * PARTS, n), F32),
        in_specs=[ANY] * len(ops),
        out_specs=pl.BlockSpec((bm, n), lambda i: (i + part * steps, 0)),
        scratch_shapes=[
            pltpu.VMEM((2, 4 * depth, bm), BF16),
            pltpu.VMEM((4 * depth, n), BF16),
            pltpu.SemaphoreType.DMA((2, 4)),
            pltpu.SemaphoreType.DMA((4,)),
        ],
        input_output_aliases=aliases,
        compiler_params=params(),
        cost_estimate=cost(m, n, 4 * depth),
        name="down_grad",
    )(*ops)


def params():
    return pltpu.CompilerParams(vmem_limit_bytes=60 << 20, dimension_semantics=("arbitrary",))


def load(copies):
    @pl.when(pl.program_id(0) == 0)
    def _():
        for c in copies:
            c.start()
        for c in copies:
            c.wait()


def place(src, dst, sem):
    return pltpu.make_async_copy(src, dst, sem)


def forward_kernel(x, x1, w, *refs):
    acts, (slope, lhs, sem) = refs[:PIECES], refs[PIECES:]
    half = x.shape[1]
    col = lax.axis_index("col")
    at = lambda k: lhs.at[:, pl.ds(pl.multiple_of(k * half, half), half)]
    load([place(x, at(col), sem.at[0]), place(x1, at(1 - col), sem.at[1])])
    u = lax.dot_general(lhs[...], w[...], NN, preferred_element_type=F32)
    cdf = 0.5 * (1.0 + lax.erf(u * INV_ROOT_TWO))
    slope[...] = cdf + u * jnp.exp(-0.5 * u * u) * INV_ROOT_TAU
    act = (u * cdf).astype(BF16)
    per = pl.num_programs(0) // PIECES
    for j, a in enumerate(acts):
        @pl.when(pl.program_id(0) // per == j)
        def _(a=a):
            a[...] = act


def forward(x, x1, w, bn=512):
    t, _ = x.shape
    h, f = w.shape
    per = f // bn // PIECES
    *acts, slope = pl.pallas_call(
        forward_kernel,
        grid=(f // bn,),
        out_shape=[jax.ShapeDtypeStruct((t, f // PIECES), BF16)] * PIECES + [jax.ShapeDtypeStruct((t, f), F32)],
        in_specs=[ANY, ANY, pl.BlockSpec((h, bn), lambda i: (0, i))],
        out_specs=[pl.BlockSpec((t, bn), lambda i, j=j: (0, jnp.clip(i - j * per, 0, per - 1))) for j in range(PIECES)]
        + [pl.BlockSpec((t, bn), lambda i: (0, i))],
        scratch_shapes=[pltpu.VMEM((t, h), BF16), pltpu.SemaphoreType.DMA((2,))],
        compiler_params=params(),
        cost_estimate=cost(t, f, h),
        name="forward",
    )(x, x1, w)
    return acts, slope


def backward_kernel(s, g, g1, wc, wa, wb, slope, out, lhs, sem):
    half = g.shape[1]
    sub = half // 2
    layer = lax.axis_index("depth")
    cut = lambda k: g1.at[:, pl.ds(pl.multiple_of(k * sub, sub), sub)]
    load([
        place(g, lhs.at[:, pl.ds(0, half)], sem.at[0]),
        place(cut(layer), lhs.at[:, pl.ds(half, sub)], sem.at[1]),
        place(cut(1 - layer), lhs.at[:, pl.ds(half + sub, sub)], sem.at[2]),
    ])
    d = lax.dot_general(lhs[:, :half], wc[...], NT, preferred_element_type=F32)
    d = d + lax.dot_general(lhs[:, half:half + sub], wa[...], NT, preferred_element_type=F32)
    d = d + lax.dot_general(lhs[:, half + sub:], wb[...], NT, preferred_element_type=F32)
    out[...] = (d * slope[...]).astype(BF16)


def backward(s, g, g1, down_g, down_a, down_b, slope, bn=512):
    t, half = g.shape
    f = slope.shape[1]
    steps = f // bn
    return pl.pallas_call(
        backward_kernel,
        grid_spec=pltpu.PrefetchScalarGridSpec(
            num_scalar_prefetch=1,
            grid=(steps,),
            in_specs=[
                ANY, ANY,
                pl.BlockSpec((bn, half), lambda i, s: (s[0] * steps + i, 0)),
                pl.BlockSpec((bn, half // 2), lambda i, s: (i, 0)),
                pl.BlockSpec((bn, half // 2), lambda i, s: (i, 0)),
                pl.BlockSpec((t, bn), lambda i, s: (0, i)),
            ],
            out_specs=pl.BlockSpec((t, bn), lambda i, s: (0, i)),
            scratch_shapes=[pltpu.VMEM((t, 2 * half), BF16), pltpu.SemaphoreType.DMA((3,))],
        ),
        out_shape=jax.ShapeDtypeStruct((t, f), BF16),
        compiler_params=params(),
        cost_estimate=cost(t, f, 2 * half),
        name="backward",
    )(s, g, g1, down_g, down_a, down_b, slope)


def row_kernel(dims, count, s, *refs):
    srcs, w, rest = refs[:count], refs[count], refs[count + 1:]
    add = rest[0] if len(rest) == 4 else None
    out, lhs, sem = rest[-3:]
    width = srcs[0].shape[1]
    load([place(x, lhs.at[:, pl.ds(k * width, width)], sem.at[k]) for k, x in enumerate(srcs)])
    r = lax.dot_general(lhs[...], w[...], dims, preferred_element_type=F32)
    if add is not None:
        r = r + add[...]
    out[...] = r.astype(out.dtype)


def row_product(s, srcs, w, add, half, dims, bn=256):
    t = srcs[0].shape[0]
    f = srcs[0].shape[1] * len(srcs)
    steps = half // bn
    if dims is NT:
        wspec = pl.BlockSpec((bn, f), lambda i, s: (s[0] * steps + i, 0))
    else:
        wspec = pl.BlockSpec((f, bn), lambda i, s: (s[0], i))
    tile = pl.BlockSpec((t, bn), lambda i, s: (0, i))
    return pl.pallas_call(
        functools.partial(row_kernel, dims, len(srcs)),
        grid_spec=pltpu.PrefetchScalarGridSpec(
            num_scalar_prefetch=1,
            grid=(steps,),
            in_specs=[ANY] * len(srcs) + [wspec] + ([] if add is None else [tile]),
            out_specs=tile,
            scratch_shapes=[pltpu.VMEM((t, f), BF16), pltpu.SemaphoreType.DMA((len(srcs),))],
        ),
        out_shape=jax.ShapeDtypeStruct((t, half), F32 if add is None else BF16),
        compiler_params=params(),
        cost_estimate=cost(t, half, f),
        name="row_product",
    )(s, *srcs, w, *([] if add is None else [add]))


def swap(x, axis):
    return lax.ppermute(x, axis, SWAP)


def solution(mesh):
    act_spec = P(("depth", "row"), "col")
    wgt_spec = P("row", "col")

    def grid_block(tok, up, down, grad):
        layer, col, row = lax.axis_index("depth"), lax.axis_index("col"), lax.axis_index("row")
        half = tok.shape[1]
        wide = up.shape[1]
        diag = row == col
        here = jnp.full((1,), col, jnp.int32)
        away = 1 - here

        q = wide // 2
        sub = lax.dynamic_slice(down, (row * q, layer * (half // 2)), (q, half // 2))
        oth = swap(lax.dynamic_slice(down, ((1 - row) * q, layer * (half // 2)), (q, half // 2)), "row")
        piece = jnp.where(diag, oth, sub)

        tok_1 = swap(tok, "col")
        tok_2 = swap(tok, "depth")
        grad_1 = swap(grad, "col")
        grad_2 = swap(grad, "depth")
        up_g = lax.all_gather(up, "row", axis=0, tiled=True)
        down_g = lax.all_gather(down, "row", axis=0, tiled=True)
        e = q // 2
        p1a, p1b = swap(piece[:e], "col"), swap(piece[e:], "col")
        p2a, p2b = swap(p1a, "depth"), swap(p1b, "depth")
        p1, p2 = jnp.concatenate([p1a, p1b], 0), jnp.concatenate([p2a, p2b], 0)
        tok_3 = swap(tok_1, "depth")
        grad_3 = swap(grad_1, "depth")
        down_a = lax.all_gather(p1, "row", axis=0, tiled=True)
        down_b = lax.all_gather(p2, "row", axis=0, tiled=True)

        act_h, slope_h = forward(tok, tok_1, up_g)
        act_t, slope_t = forward(tok_2, tok_3, up_g)
        imp_h = [swap(act_h[j], "col") for j in range(PIECES)]
        imp_t = [swap(imp_h[j], "depth") for j in range(PIECES)]

        du_h = backward(here, grad, grad_1, down_g, down_a, down_b, slope_h)
        sent = swap(row_product(away, [du_h], up_g, None, half, NT), "col")
        grad_tok = row_product(here, [du_h], up_g, sent, half, NT)
        du_t = backward(here, grad_2, grad_3, down_g, down_a, down_b, slope_t)

        pick = lambda a, b, k: jnp.where(k == col, a, b)
        flip = lambda x: jnp.swapaxes(x, 0, 1)
        tok_mh, tok_mt = flip(pick(tok, tok_1, row)), flip(pick(tok_2, tok_3, row))
        tok_sh = swap(flip(pick(tok, tok_1, 1 - row)), "row")
        tok_st = swap(flip(pick(tok_2, tok_3, 1 - row)), "row")
        du_sh, du_st = swap(du_h, "row"), swap(du_t, "row")
        up_sum = up_grad([tok_mh, tok_mt, tok_sh, tok_st], [du_h, du_t, du_sh, du_st])

        out = row_product(here, act_h, down_g, None, half, NN)
        out = row_product(away, imp_h, down_g, out, half, NN)

        grads = [grad, swap(grad, "row"), grad_2, swap(grad_2, "row")]
        oth_h = [swap(jnp.where(diag, imp_h[j], act_h[j]), "row") for j in range(PIECES)]
        oth_t = [swap(jnp.where(diag, imp_t[j], act_t[j]), "row") for j in range(PIECES)]
        down_sum = None
        per = PIECES // PARTS
        for n in range(PARTS):
            cut = lambda xs: xs[n * per:(n + 1) * per]
            down_sum = down_grad(cut(act_h), cut(act_t), cut(imp_h), cut(imp_t), cut(oth_h), cut(oth_t), grads, n, down_sum)
        return out, grad_tok, up_sum, down_sum

    return jax.shard_map(grid_block, mesh=mesh, in_specs=(act_spec, wgt_spec, wgt_spec, act_spec), out_specs=(act_spec, act_spec, wgt_spec, wgt_spec), check_vma=False)
```

time: 2240 us -> 1790 us (0.80)
  matrix products: 1030 us -> 0 us
  Pallas kernels: 0 us -> 847 us
  waiting for transfers between devices: 1000 us -> 784 us
  local copies, waits for them, and re-layouts: 68.9 us -> 34.5 us
    dot_general x19 -> x0, matrix products: 1030 us -> none  [the longest x15 788 us: dot(): out = jnp.einsum(eq, a, b, preferred_element_type=jnp.float32)]
    pallas_call x0 -> x11, Pallas kernels: none -> 847 us  [the longest x2 186 us: forward(): pl.pallas_call(forward_kernel, grid=(f // bn,), out_shape=[jax.ShapeDtype...]
    ppermute x28 -> x34, waiting for transfers between devices: 1000 us -> 782 us  [swap(): return lax.ppermute(x, axis, SWAP)]
    unnamed x16 -> x10, local copies, waits for them, and re-layouts: 27.7 us -> 0.02 us
  transfers between devices with their start and end apart: 32 -> 38, of which waited for: 14 -> 11; matrix products, arithmetic and copies ran while one was open for 44% -> 6% of each run, Pallas kernels for 0% -> 39%
where the time goes in v2:
time: 1790 us
  Pallas kernels  847 us (47%)
  waiting for transfers between devices  784 us (44%)
  other arithmetic  78.3 us (4%)
  local copies, waits for them, and re-layouts  34.5 us (2%)
  starting transfers between devices  28.4 us (2%)
    ppermute x34, waiting for transfers between devices, swap(): return lax.ppermute(x, axis, SWAP)  782 us
    pallas_call x2, Pallas kernels, forward(): pl.pallas_call(forward_kernel, grid=(f // bn,), out_shape=[jax.ShapeDtype...  186 us
    pallas_call x4, Pallas kernels, row_product(): pl.pallas_call(functools.partial(row_kernel, dims, len(srcs)), grid_spec=...  184 us
    pallas_call x2, Pallas kernels, backward(): pl.pallas_call(backward_kernel, grid_spec=pltpu.PrefetchScalarGridSpec(nu...  163 us
    pallas_call x2, Pallas kernels, down_grad(): pl.pallas_call(functools.partial(down_kernel, pieces), grid=(steps,), out...  161 us
    pallas_call x1, Pallas kernels, up_grad(): pl.pallas_call(up_kernel, grid=(n // bn,), out_shape=jax.ShapeDtypeStruct...  154 us
  transfers between devices with their start and end apart: 38, of which 11 were waited for; matrix products, arithmetic and copies ran while one was open for 6% of the time, Pallas kernels for 39%

profile of v2, /device:TPU:0, one launch (start us, length us, event | category | flops | bytes accessed | tf_op | source)
XLA Modules:
  0.0 1786.5 jit_solution(7471541531052017535)
XLA Ops:
  8.0 7.8 dynamic_slice.6
  16.9 13.1 collective-permute-done.6
  30.0 13.2 dynamic-slice_select_fusion
  46.3 90.2 %collective-permute-done.8 = bf16[2048,1024]{1,0:T(8,128)(2,1)} collective-permute-done((bf16[2048,1024]{1,0:T(8,128)(2,1)S(1)}, bf16[2048,1024]{1,0:T(8,128)(2,1)}, u32[]{:S(2)}, u32[]{:S(2)}) %collective-permute-start.8) | collective-permute-done | bytes 4194336 | tf_op jit(solution)/shard_map/ppermute | solution.py:275
  136.5 89.9 %collective-permute-done.7 = bf16[2048,1024]{1,0:T(8,128)(2,1)} collective-permute-done((bf16[2048,1024]{1,0:T(8,128)(2,1)S(1)}, bf16[2048,1024]{1,0:T(8,128)(2,1)}, u32[]{:S(2)}, u32[]{:S(2)}) %collective-permute-start.7) | collective-permute-done | bytes 4194336 | tf_op jit(solution)/shard_map/ppermute | solution.py:275
  226.4 7.8 pad_maximum_fusion
  238.5 91.7 %collective-permute-done.10 = bf16[2048,1024]{1,0:T(8,128)(2,1)} collective-permute-done((bf16[2048,1024]{1,0:T(8,128)(2,1)}, bf16[2048,1024]{1,0:T(8,128)(2,1)}, u32[]{:S(2)}, u32[]{:S(2)}) %collective-permute-start.10) | collective-permute-done | bytes 4194336 | tf_op jit(solution)/shard_map/ppermute | solution.py:275
  330.2 88.3 %collective-permute-done.9 = bf16[2048,1024]{1,0:T(8,128)(2,1)} collective-permute-done((bf16[2048,1024]{1,0:T(8,128)(2,1)}, bf16[2048,1024]{1,0:T(8,128)(2,1)}, u32[]{:S(2)}, u32[]{:S(2)}) %collective-permute-start.9) | collective-permute-done | bytes 4194336 | tf_op jit(solution)/shard_map/ppermute | solution.py:275
  418.4 7.7 pad_maximum_fusion.1
  430.3 89.2 %collective-permute-done.x1 = bf16[1024,2048]{1,0:T(8,128)(2,1)} collective-permute-done((bf16[1024,2048]{1,0:T(8,128)(2,1)}, bf16[1024,2048]{1,0:T(8,128)(2,1)}, u32[]{:S(2)}, u32[]{:S(2)}) %collective-permute-start) | collective-permute-done | bytes 4194336 | tf_op jit(solution)/shard_map/ppermute | solution.py:275
  522.8 6.0 select_bitcast_fusion.1
  528.8 82.7 %collective-permute-done.13.x1 = bf16[1024,2048]{1,0:T(8,128)(2,1)} collective-permute-done((bf16[1024,2048]{1,0:T(8,128)(2,1)}, bf16[1024,2048]{1,0:T(8,128)(2,1)}, u32[]{:S(2)}, u32[]{:S(2)}) %collective-permute-start.13) | collective-permute-done | bytes 4194336 | tf_op jit(solution)/shard_map/ppermute | solution.py:275
  611.5 5.8 select_bitcast_fusion
  618.7 6.4 copy.9.x0
  626.0 6.5 copy.10.x1
  632.4 6.4 copy.11.x2
  638.9 6.4 copy.12.x3
  645.3 92.8 %forward.2 = (bf16[1024,2048]{1,0:T(8,128)(2,1)}, bf16[1024,2048]{1,0:T(8,128)(2,1)}, bf16[1024,2048]{1,0:T(8,128)(2,1)}, bf16[1024,2048]{1,0:T(8,128)(2,1)}, f32[1024,8192]{1,0:T(8,128)}) custom-call(bf16[1024,2048]{1,0:T(8,128)(2,1)} %x.1, bf16[1024,2048]{1,0:T(8,128)(2,1)} %collective-permute-done.x1, ...), custom_call_target="tpu_custom_call" | custom-call | flops 68719476736 | bytes 109051904 | tf_op jit(solution)/shard_map/forward/pallas_call | solution.py:180
  740.1 92.8 %forward.3 = (bf16[1024,2048]{1,0:T(8,128)(2,1)}, bf16[1024,2048]{1,0:T(8,128)(2,1)}, bf16[1024,2048]{1,0:T(8,128)(2,1)}, bf16[1024,2048]{1,0:T(8,128)(2,1)}, f32[1024,8192]{1,0:T(8,128)}) custom-call(bf16[1024,2048]{1,0:T(8,128)(2,1)} %collective-permute-done.12.x, bf16[1024,2048]{1,0:T(8,128)(2,1)} %collective-permute-done.13.x1, ...), custom_call_target="tpu_custom_call" | custom-call | flops 68719476736 | bytes 109051904 | tf_op jit(solution)/shard_map/forward/pallas_call | solution.py:180
  833.0 81.7 %backward.2.refs_0_.d0 = bf16[1024,8192]{1,0:T(8,128)(2,1)} custom-call(s32[1]{0:T(128)} %bitcast.s, bf16[1024,2048]{1,0:T(8,128)(2,1)} %refs_12_.3, bf16[1024,2048]{1,0:T(8,128)(2,1)} %collective-permute-done.5.g1, bf16[16384,2048]{1,0:T(8,128)(2,1)} %all-gather.7.cloned.1.call-done.refs_4_.wc, bf16[8192,1024]{1,0:T(8,128)(2,1)} %all-gather.9.cloned.1.call-done.wa, ...), custom_call_target="tpu_custom_call" | custom-call | flops 68719476736 | bytes 109051904 | tf_op jit(solution)/shard_map/backward/pallas_call | solution.py:215
  916.8 81.5 %backward.3.d1 = bf16[1024,8192]{1,0:T(8,128)(2,1)} custom-call(s32[1]{0:T(128)} %bitcast.s, bf16[1024,2048]{1,0:T(8,128)(2,1)} %collective-permute-done.16.g.refs_14_, bf16[1024,2048]{1,0:T(8,128)(2,1)} %collective-permute-done.17.g1, bf16[16384,2048]{1,0:T(8,128)(2,1)} %all-gather.7.cloned.1.call-done.refs_4_.wc, ...), custom_call_target="tpu_custom_call" | custom-call | flops 68719476736 | bytes 109051904 | tf_op jit(solution)/shard_map/backward/pallas_call | solution.py:215
  998.2 45.8 %row_product.6 = f32[1024,2048]{1,0:T(8,128)} custom-call(s32[1]{0:T(128)S(6)} %sub.8.s, bf16[1024,8192]{1,0:T(8,128)(2,1)} %backward.2.refs_0_.d0, bf16[4096,8192]{1,0:T(8,128)(2,1)} %all-gather.5.cloned.1.call-done.w.refs_1_), custom_call_target="tpu_custom_call" | custom-call | flops 34359738368 | bytes 58720256 | tf_op jit(solution)/shard_map/row_product/pallas_call | solution.py:258
  1046.9 54.6 %collective-permute-done.4.refs_3_.refs_5_ = bf16[1024,2048]{1,0:T(8,128)(2,1)} collective-permute-done((bf16[1024,2048]{1,0:T(8,128)(2,1)}, bf16[1024,2048]{1,0:T(8,128)(2,1)}, u32[]{:S(2)}, u32[]{:S(2)}) %collective-permute-start.4) | collective-permute-done | bytes 4194336 | tf_op jit(solution)/shard_map/ppermute | solution.py:275
  1102.7 46.0 %row_product.4.refs_5_ = f32[1024,2048]{1,0:T(8,128)} custom-call(s32[1]{0:T(128)} %bitcast.s, bf16[1024,2048]{1,0:T(8,128)(2,1)} %get-tuple-element.14.refs_0_, bf16[1024,2048]{1,0:T(8,128)(2,1)} %get-tuple-element.15.refs_1_, bf16[1024,2048]{1,0:T(8,128)(2,1)} %get-tuple-element.16.refs_2_.refs_0_, bf16[1024,2048]{1,0:T(8,128)(2,1)} %get-tuple-element.17.refs_3_.refs_1_, ...), custom_call_target="tpu_custom_call" | custom-call | flops 34359738368 | bytes 58720256 | tf_op jit(solution)/shard_map/row_product/pallas_call | solution.py:258
  1169.0 60.4 %collective-permute-done.29.refs_7_ = bf16[1024,2048]{1,0:T(8,128)(2,1)} collective-permute-done((bf16[1024,2048]{1,0:T(8,128)(2,1)}, bf16[1024,2048]{1,0:T(8,128)(2,1)}, u32[]{:S(2)}, u32[]{:S(2)}) %collective-permute-start.29) | collective-permute-done | bytes 4194336 | tf_op jit(solution)/shard_map/ppermute | solution.py:275
  1230.6 46.1 %row_product.5 = bf16[1024,2048]{1,0:T(8,128)(2,1)} custom-call(s32[1]{0:T(128)S(6)} %sub.8.s, bf16[1024,2048]{1,0:T(8,128)(2,1)} %collective-permute-done.1.refs_0_.refs_4_, bf16[1024,2048]{1,0:T(8,128)(2,1)} %collective-permute-done.2.refs_1_.refs_5_, bf16[1024,2048]{1,0:T(8,128)(2,1)} %collective-permute-done.3.refs_2_.refs_4_, ...), custom_call_target="tpu_custom_call" | custom-call | flops 34359738368 | bytes 58720256 | tf_op jit(solution)/shard_map/row_product/pallas_call | solution.py:258
  1286.1 33.2 %collective-permute-done.20.refs_6_ = bf16[1024,2048]{1,0:T(8,128)(2,1)} collective-permute-done((bf16[1024,2048]{1,0:T(8,128)(2,1)}, bf16[1024,2048]{1,0:T(8,128)(2,1)}, u32[]{:S(2)}, u32[]{:S(2)}) %collective-permute-start.20) | collective-permute-done | bytes 4194336 | tf_op jit(solution)/shard_map/ppermute | solution.py:275
  1319.3 89.1 %collective-permute-done.21.refs_7_ = bf16[1024,2048]{1,0:T(8,128)(2,1)} collective-permute-done((bf16[1024,2048]{1,0:T(8,128)(2,1)}, bf16[1024,2048]{1,0:T(8,128)(2,1)}, u32[]{:S(2)}, u32[]{:S(2)}) %collective-permute-start.21) | collective-permute-done | bytes 4194336 | tf_op jit(solution)/shard_map/ppermute | solution.py:275
  1408.9 46.2 %row_product.7 = bf16[1024,2048]{1,0:T(8,128)(2,1)} custom-call(s32[1]{0:T(128)} %bitcast.s, bf16[1024,8192]{1,0:T(8,128)(2,1)} %backward.2.refs_0_.d0, bf16[4096,8192]{1,0:T(8,128)(2,1)} %all-gather.5.cloned.1.call-done.w.refs_1_, f32[1024,2048]{1,0:T(8,128)} %collective-permute-done.11.refs_2_), custom_call_target="tpu_custom_call" | custom-call | flops 34359738368 | bytes 58720256 | tf_op jit(solution)/shard_map/row_product/pallas_call | solution.py:258
  1465.1 80.5 %down_grad.2.refs_16_ = f32[8192,2048]{1,0:T(8,128)} custom-call(bf16[1024,2048]{1,0:T(8,128)(2,1)} %get-tuple-element.14.refs_0_, bf16[1024,2048]{1,0:T(8,128)(2,1)} %get-tuple-element.15.refs_1_, bf16[1024,2048]{1,0:T(8,128)(2,1)} %get-tuple-element.22.refs_2_, bf16[1024,2048]{1,0:T(8,128)(2,1)} %get-tuple-element.23.refs_3_, ...), custom_call_target="tpu_custom_call" | custom-call | flops 68719476736 | bytes 83886080 | tf_op jit(solution)/shard_map/down_grad/pallas_call | solution.py:123
  1545.7 80.4 %down_grad.3 = f32[8192,2048]{1,0:T(8,128)} custom-call(bf16[1024,2048]{1,0:T(8,128)(2,1)} %get-tuple-element.16.refs_2_.refs_0_, bf16[1024,2048]{1,0:T(8,128)(2,1)} %get-tuple-element.17.refs_3_.refs_1_, bf16[1024,2048]{1,0:T(8,128)(2,1)} %get-tuple-element.20.refs_2_, ...), custom_call_target="tpu_custom_call", output_to_operand_aliasing={{}: (16, {})} | custom-call | flops 68719476736 | bytes 83886080 | tf_op jit(solution)/shard_map/down_grad/pallas_call | solution.py:123
  1626.1 153.6 %up_grad.1 = f32[2048,8192]{1,0:T(8,128)} custom-call(bf16[2048,1024]{1,0:T(8,128)(2,1)} %copy.9.x0, bf16[2048,1024]{1,0:T(8,128)(2,1)} %copy.10.x1, bf16[2048,1024]{1,0:T(8,128)(2,1)} %copy.11.x2, bf16[2048,1024]{1,0:T(8,128)(2,1)} %copy.12.x3, bf16[1024,8192]{1,0:T(8,128)(2,1)} %backward.2.refs_0_.d0, bf16[1024,8192]{1,0:T(8,128)(2,1)} %backward.3.d1, ...), custom_call_target="tpu_custom_call" | custom-call | flops 137438953472 | bytes 150994944 | tf_op jit(solution)/shard_map/up_grad/pallas_call | solution.py:50
  (88 shorter events, 68.5 us)
Async XLA Ops:
  7.2 638.1 %all-gather.5.cloned.1.call-start = ((), (), s32[]{:S(2)}) async-start(), calls=%async_computation | async-start | bytes 100663296 | tf_op jit(solution)/shard_map/all_gather | solution.py:299
  7.9 825.1 %all-gather.9.cloned.1.call-start = ((), (), s32[]{:S(2)}) async-start(), calls=%async_computation.2 | async-start | bytes 25165824 | tf_op jit(solution)/shard_map/all_gather | solution.py:307
  44.2 92.3 %collective-permute-start.8 = (bf16[2048,1024]{1,0:T(8,128)(2,1)S(1)}, bf16[2048,1024]{1,0:T(8,128)(2,1)}, u32[]{:S(2)}, u32[]{:S(2)}) collective-permute-start(bf16[2048,1024]{1,0:T(8,128)(2,1)S(1)} %get-tuple-element.29), channel_id=1, source_target_pairs={{0,2},{2,0},{1,3},{3,1},{4,6},{6,4},{5,7},{7,5}} | collective-permute-start | bytes 12582920 | tf_op jit(solution)/shard_map/ppermute | solution.py:275
  44.3 182.1 %collective-permute-start.7 = (bf16[2048,1024]{1,0:T(8,128)(2,1)S(1)}, bf16[2048,1024]{1,0:T(8,128)(2,1)}, u32[]{:S(2)}, u32[]{:S(2)}) collective-permute-start(bf16[2048,1024]{1,0:T(8,128)(2,1)S(1)} %get-tuple-element.28), channel_id=1, source_target_pairs={{0,2},{2,0},{1,3},{3,1},{4,6},{6,4},{5,7},{7,5}} | collective-permute-start | bytes 12582920 | tf_op jit(solution)/shard_map/ppermute | solution.py:275
  234.2 598.8 %all-gather.11.cloned.1.call-start = ((), (), s32[]{:S(2)}) async-start(), calls=%async_computation.3 | async-start | bytes 25165824 | tf_op jit(solution)/shard_map/all_gather | solution.py:308
  234.2 95.9 %collective-permute-start.10 = (bf16[2048,1024]{1,0:T(8,128)(2,1)}, bf16[2048,1024]{1,0:T(8,128)(2,1)}, u32[]{:S(2)}, u32[]{:S(2)}) collective-permute-start(bf16[2048,1024]{1,0:T(8,128)(2,1)} %collective-permute-done.8), channel_id=1, source_target_pairs={{0,4},{4,0},{1,5},{5,1},{2,6},{6,2},{3,7},{7,3}} | collective-permute-start | bytes 12582920 | tf_op jit(solution)/shard_map/ppermute | solution.py:275
  238.4 180.0 %collective-permute-start.9 = (bf16[2048,1024]{1,0:T(8,128)(2,1)}, bf16[2048,1024]{1,0:T(8,128)(2,1)}, u32[]{:S(2)}, u32[]{:S(2)}) collective-permute-start(bf16[2048,1024]{1,0:T(8,128)(2,1)} %collective-permute-done.7), channel_id=1, source_target_pairs={{0,4},{4,0},{1,5},{5,1},{2,6},{6,2},{3,7},{7,3}} | collective-permute-start | bytes 12582920 | tf_op jit(solution)/shard_map/ppermute | solution.py:275
  426.2 406.8 %all-gather.7.cloned.1.call-start = ((), (), s32[]{:S(2)}) async-start(), calls=%async_computation.1 | async-start | bytes 100663296 | tf_op jit(solution)/shard_map/all_gather | solution.py:300
  426.8 92.8 %collective-permute-start = (bf16[1024,2048]{1,0:T(8,128)(2,1)}, bf16[1024,2048]{1,0:T(8,128)(2,1)}, u32[]{:S(2)}, u32[]{:S(2)}) collective-permute-start(bf16[1024,2048]{1,0:T(8,128)(2,1)} %x.1), channel_id=1, source_target_pairs={{0,2},{2,0},{1,3},{3,1},{4,6},{6,4},{5,7},{7,5}} | collective-permute-start | bytes 12582920 | tf_op jit(solution)/shard_map/ppermute | solution.py:275
  428.6 100.2 %collective-permute-start.12 = (bf16[1024,2048]{1,0:T(8,128)(2,1)}, bf16[1024,2048]{1,0:T(8,128)(2,1)}, u32[]{:S(2)}, u32[]{:S(2)}) collective-permute-start(bf16[1024,2048]{1,0:T(8,128)(2,1)} %x.1), channel_id=1, source_target_pairs={{0,4},{4,0},{1,5},{5,1},{2,6},{6,2},{3,7},{7,3}} | collective-permute-start | bytes 12582920 | tf_op jit(solution)/shard_map/ppermute | solution.py:275
  519.6 91.9 %collective-permute-start.13 = (bf16[1024,2048]{1,0:T(8,128)(2,1)}, bf16[1024,2048]{1,0:T(8,128)(2,1)}, u32[]{:S(2)}, u32[]{:S(2)}) collective-permute-start(bf16[1024,2048]{1,0:T(8,128)(2,1)} %collective-permute-done.x1), channel_id=1, source_target_pairs={{0,4},{4,0},{1,5},{5,1},{2,6},{6,2},{3,7},{7,3}} | collective-permute-start | bytes 12582920 | tf_op jit(solution)/shard_map/ppermute | solution.py:275
  521.0 104.1 %collective-permute-start.5 = (bf16[1024,2048]{1,0:T(8,128)(2,1)}, bf16[1024,2048]{1,0:T(8,128)(2,1)}, u32[]{:S(2)}, u32[]{:S(2)}) collective-permute-start(bf16[1024,2048]{1,0:T(8,128)(2,1)} %refs_12_.3), channel_id=1, source_target_pairs={{0,2},{2,0},{1,3},{3,1},{4,6},{6,4},{5,7},{7,5}} | collective-permute-start | bytes 12582920 | tf_op jit(solution)/shard_map/ppermute | solution.py:275
  528.7 103.7 %collective-permute-start.14 = (bf16[2048,1024]{0,1:T(8,128)(2,1)}, bf16[2048,1024]{0,1:T(8,128)(2,1)}, u32[]{:S(2)}, u32[]{:S(2)}) collective-permute-start(bf16[2048,1024]{0,1:T(8,128)(2,1)} %get-tuple-element.26), channel_id=1, source_target_pairs={{0,1},{1,0},{2,3},{3,2},{4,5},{5,4},{6,7},{7,6}} | collective-permute-start | bytes 12582920 | tf_op jit(solution)/shard_map/ppermute | solution.py:275
  617.3 297.4 %collective-permute-start.16 = (bf16[1024,2048]{1,0:T(8,128)(2,1)}, bf16[1024,2048]{1,0:T(8,128)(2,1)}, u32[]{:S(2)}, u32[]{:S(2)}) collective-permute-start(bf16[1024,2048]{1,0:T(8,128)(2,1)} %refs_12_.3), channel_id=1, source_target_pairs={{0,4},{4,0},{1,5},{5,1},{2,6},{6,2},{3,7},{7,3}} | collective-permute-start | bytes 12582920 | tf_op jit(solution)/shard_map/ppermute | solution.py:275
  618.5 549.1 %collective-permute-start.26 = (bf16[1024,2048]{1,0:T(8,128)(2,1)}, bf16[1024,2048]{1,0:T(8,128)(2,1)}, u32[]{:S(2)}, u32[]{:S(2)}) collective-permute-start(bf16[1024,2048]{1,0:T(8,128)(2,1)} %refs_12_.3), channel_id=1, source_target_pairs={{0,1},{1,0},{2,3},{3,2},{4,5},{5,4},{6,7},{7,6}} | collective-permute-start | bytes 12582920 | tf_op jit(solution)/shard_map/ppermute | solution.py:275
  625.1 291.3 %collective-permute-start.17 = (bf16[1024,2048]{1,0:T(8,128)(2,1)}, bf16[1024,2048]{1,0:T(8,128)(2,1)}, u32[]{:S(2)}, u32[]{:S(2)}) collective-permute-start(bf16[1024,2048]{1,0:T(8,128)(2,1)} %collective-permute-done.5.g1), channel_id=1, source_target_pairs={{0,4},{4,0},{1,5},{5,1},{2,6},{6,2},{3,7},{7,3}} | collective-permute-start | bytes 12582920 | tf_op jit(solution)/shard_map/ppermute | solution.py:275
  738.1 305.9 %collective-permute-start.1 = (bf16[1024,2048]{1,0:T(8,128)(2,1)}, bf16[1024,2048]{1,0:T(8,128)(2,1)}, u32[]{:S(2)}, u32[]{:S(2)}) collective-permute-start(bf16[1024,2048]{1,0:T(8,128)(2,1)} %get-tuple-element.14.refs_0_), channel_id=1, source_target_pairs={{0,2},{2,0},{1,3},{3,1},{4,6},{6,4},{5,7},{7,5}} | collective-permute-start | bytes 12582920 | tf_op jit(solution)/shard_map/ppermute | solution.py:275
  739.8 304.3 %collective-permute-start.2 = (bf16[1024,2048]{1,0:T(8,128)(2,1)}, bf16[1024,2048]{1,0:T(8,128)(2,1)}, u32[]{:S(2)}, u32[]{:S(2)}) collective-permute-start(bf16[1024,2048]{1,0:T(8,128)(2,1)} %get-tuple-element.15.refs_1_), channel_id=1, source_target_pairs={{0,2},{2,0},{1,3},{3,1},{4,6},{6,4},{5,7},{7,5}} | collective-permute-start | bytes 12582920 | tf_op jit(solution)/shard_map/ppermute | solution.py:275
  914.7 131.0 %collective-permute-start.3 = (bf16[1024,2048]{1,0:T(8,128)(2,1)}, bf16[1024,2048]{1,0:T(8,128)(2,1)}, u32[]{:S(2)}, u32[]{:S(2)}) collective-permute-start(bf16[1024,2048]{1,0:T(8,128)(2,1)} %get-tuple-element.16.refs_2_.refs_0_), channel_id=1, source_target_pairs={{0,2},{2,0},{1,3},{3,1},{4,6},{6,4},{5,7},{7,5}} | collective-permute-start | bytes 12582920 | tf_op jit(solution)/shard_map/ppermute | solution.py:275
  916.4 185.1 %collective-permute-start.4 = (bf16[1024,2048]{1,0:T(8,128)(2,1)}, bf16[1024,2048]{1,0:T(8,128)(2,1)}, u32[]{:S(2)}, u32[]{:S(2)}) collective-permute-start(bf16[1024,2048]{1,0:T(8,128)(2,1)} %get-tuple-element.17.refs_3_.refs_1_), channel_id=1, source_target_pairs={{0,2},{2,0},{1,3},{3,1},{4,6},{6,4},{5,7},{7,5}} | collective-permute-start | bytes 12582920 | tf_op jit(solution)/shard_map/ppermute | solution.py:275
  1044.0 123.6 %collective-permute-start.27 = (bf16[1024,2048]{1,0:T(8,128)(2,1)}, bf16[1024,2048]{1,0:T(8,128)(2,1)}, u32[]{:S(2)}, u32[]{:S(2)}) collective-permute-start(bf16[1024,2048]{1,0:T(8,128)(2,1)} %collective-permute-done.16.g.refs_14_), channel_id=1, source_target_pairs={{0,1},{1,0},{2,3},{3,2},{4,5},{5,4},{6,7},{7,6}} | collective-permute-start | bytes 12582920 | tf_op jit(solution)/shard_map/ppermute | solution.py:275
  1044.1 242.0 %collective-permute-start.11 = (f32[1024,2048]{1,0:T(8,128)}, f32[1024,2048]{1,0:T(8,128)}, u32[]{:S(2)}, u32[]{:S(2)}) collective-permute-start(f32[1024,2048]{1,0:T(8,128)} %row_product.6), channel_id=1, source_target_pairs={{0,2},{2,0},{1,3},{3,1},{4,6},{6,4},{5,7},{7,5}} | collective-permute-start | bytes 25165832 | tf_op jit(solution)/shard_map/ppermute | solution.py:275
  1045.8 122.4 %collective-permute-start.28 = (bf16[1024,2048]{1,0:T(8,128)(2,1)}, bf16[1024,2048]{1,0:T(8,128)(2,1)}, u32[]{:S(2)}, u32[]{:S(2)}) collective-permute-start(bf16[1024,2048]{1,0:T(8,128)(2,1)} %collective-permute-done.1.refs_0_.refs_4_), channel_id=1, source_target_pairs={{0,4},{4,0},{1,5},{5,1},{2,6},{6,2},{3,7},{7,3}} | collective-permute-start | bytes 12582920 | tf_op jit(solution)/shard_map/ppermute | solution.py:275
  1101.5 127.9 %collective-permute-start.29 = (bf16[1024,2048]{1,0:T(8,128)(2,1)}, bf16[1024,2048]{1,0:T(8,128)(2,1)}, u32[]{:S(2)}, u32[]{:S(2)}) collective-permute-start(bf16[1024,2048]{1,0:T(8,128)(2,1)} %collective-permute-done.2.refs_1_.refs_5_), channel_id=1, source_target_pairs={{0,4},{4,0},{1,5},{5,1},{2,6},{6,2},{3,7},{7,3}} | collective-permute-start | bytes 12582920 | tf_op jit(solution)/shard_map/ppermute | solution.py:275
  1167.6 240.8 %collective-permute-start.22 = (bf16[1024,2048]{1,0:T(8,128)(2,1)}, bf16[1024,2048]{1,0:T(8,128)(2,1)}, u32[]{:S(2)}, u32[]{:S(2)}) collective-permute-start(bf16[1024,2048]{1,0:T(8,128)(2,1)} %broadcast_select_fusion.7), channel_id=1, source_target_pairs={{0,1},{1,0},{2,3},{3,2},{4,5},{5,4},{6,7},{7,6}} | collective-permute-start | bytes 12582920 | tf_op jit(solution)/shard_map/ppermute | solution.py:275
  1167.6 241.3 %collective-permute-start.30 = (bf16[1024,2048]{1,0:T(8,128)(2,1)}, bf16[1024,2048]{1,0:T(8,128)(2,1)}, u32[]{:S(2)}, u32[]{:S(2)}) collective-permute-start(bf16[1024,2048]{1,0:T(8,128)(2,1)} %broadcast_select_fusion.3), channel_id=1, source_target_pairs={{0,1},{1,0},{2,3},{3,2},{4,5},{5,4},{6,7},{7,6}} | collective-permute-start | bytes 12582920 | tf_op jit(solution)/shard_map/ppermute | solution.py:275
  1168.2 151.1 %collective-permute-start.20 = (bf16[1024,2048]{1,0:T(8,128)(2,1)}, bf16[1024,2048]{1,0:T(8,128)(2,1)}, u32[]{:S(2)}, u32[]{:S(2)}) collective-permute-start(bf16[1024,2048]{1,0:T(8,128)(2,1)} %collective-permute-done.3.refs_2_.refs_4_), channel_id=1, source_target_pairs={{0,4},{4,0},{1,5},{5,1},{2,6},{6,2},{3,7},{7,3}} | collective-permute-start | bytes 12582920 | tf_op jit(solution)/shard_map/ppermute | solution.py:275
  1229.4 179.0 %collective-permute-start.21 = (bf16[1024,2048]{1,0:T(8,128)(2,1)}, bf16[1024,2048]{1,0:T(8,128)(2,1)}, u32[]{:S(2)}, u32[]{:S(2)}) collective-permute-start(bf16[1024,2048]{1,0:T(8,128)(2,1)} %collective-permute-done.4.refs_3_.refs_5_), channel_id=1, source_target_pairs={{0,4},{4,0},{1,5},{5,1},{2,6},{6,2},{3,7},{7,3}} | collective-permute-start | bytes 12582920 | tf_op jit(solution)/shard_map/ppermute | solution.py:275
  1286.1 340.0 %collective-permute-start.18 = (bf16[1024,8192]{1,0:T(8,128)(2,1)}, bf16[1024,8192]{1,0:T(8,128)(2,1)}, u32[]{:S(2)}, u32[]{:S(2)}) collective-permute-start(bf16[1024,8192]{1,0:T(8,128)(2,1)} %backward.2.refs_0_.d0), channel_id=1, source_target_pairs={{0,1},{1,0},{2,3},{3,2},{4,5},{5,4},{6,7},{7,6}} | collective-permute-start | bytes 50331656 | tf_op jit(solution)/shard_map/ppermute | solution.py:275
  1319.3 306.8 %collective-permute-start.19 = (bf16[1024,8192]{1,0:T(8,128)(2,1)}, bf16[1024,8192]{1,0:T(8,128)(2,1)}, u32[]{:S(2)}, u32[]{:S(2)}) collective-permute-start(bf16[1024,8192]{1,0:T(8,128)(2,1)} %backward.3.d1), channel_id=1, source_target_pairs={{0,1},{1,0},{2,3},{3,2},{4,5},{5,4},{6,7},{7,6}} | collective-permute-start | bytes 50331656 | tf_op jit(solution)/shard_map/ppermute | solution.py:275
  1464.6 81.0 %collective-permute-start.23 = (bf16[1024,2048]{1,0:T(8,128)(2,1)}, bf16[1024,2048]{1,0:T(8,128)(2,1)}, u32[]{:S(2)}, u32[]{:S(2)}) collective-permute-start(bf16[1024,2048]{1,0:T(8,128)(2,1)} %broadcast_select_fusion.6), channel_id=1, source_target_pairs={{0,1},{1,0},{2,3},{3,2},{4,5},{5,4},{6,7},{7,6}} | collective-permute-start | bytes 12582920 | tf_op jit(solution)/shard_map/ppermute | solution.py:275
  1464.6 81.0 %collective-permute-start.24 = (bf16[1024,2048]{1,0:T(8,128)(2,1)}, bf16[1024,2048]{1,0:T(8,128)(2,1)}, u32[]{:S(2)}, u32[]{:S(2)}) collective-permute-start(bf16[1024,2048]{1,0:T(8,128)(2,1)} %broadcast_select_fusion.5), channel_id=1, source_target_pairs={{0,1},{1,0},{2,3},{3,2},{4,5},{5,4},{6,7},{7,6}} | collective-permute-start | bytes 12582920 | tf_op jit(solution)/shard_map/ppermute | solution.py:275
  (11 other events, 309.0 us)
Sparse Core Ops, SparseCore 0:
  9.5 94.8 all-gather.4
  234.3 29.9 all-gather.8
  426.3 28.7 all-gather.10
  456.5 99.2 all-gather.6
